TPU v7x, 128 devices: a whole 4x4x4 slice. The times are simulated.
128 devices in a mesh: patch: 128 (over y, z, x, core).
Axes of the slice: x: 4, y: 4, z: 4, core: 2. Of those that a mesh axis runs over, the one named last changes fastest.
Arguments:
- positions: float32 [3, 262144], P(None, 'patch'), may hold values from -6 to 6
- densities: float32 [3, 262144], P(None, 'patch'), may hold values from -6 to 6
- near_src: int32 [2048, 8], P('patch'), may hold values from 0 to 2047, as said below
- near_count: int32 [2048], P('patch'), may hold values from 1 to 8
- far_slot: int32 [2048, 32], P('patch'), may hold values from 0 to 511
- far_class: int32 [2048, 32], P('patch'), may hold values from 0 to 188
- far_count: int32 [2048], P('patch'), may hold values from 1 to 32
- requests: int32 [128, 128, 4], P('patch'), may hold values from 0 to 15, as said below
- up_basis: bfloat16 [2048, 144, 384], P('patch'), may hold values from -0.3125 to 0.3125
- transfer_table: bfloat16 [189, 20736], replicated, may hold values from -0.5 to 0.5
- down_basis: bfloat16 [2048, 144, 9, 128], P('patch'), may hold values from -0.09375 to 0.09375
Outputs:
- shape_grad: float32 [3, 262144], P(None, 'patch')
Inputs may be any that keep to these rules, and one draw needn't show every extreme that they name: `near_src`: the source leaf of each near-field block is held by the device of its target leaf or by the device just before or after it along patch. `requests`: each row names 4 different leaves of the source device, by their index on that device.
All inputs are finite; a program needn't handle non-finite values.
Results may differ from a plain program's by a relative error of at most 0.0042.
Values may be sent and summed in bfloat16 or wider, within the bound.
A program may use at most 192 MiB of HBM per device.

v0:
```python
import math

import jax
import jax.numpy as jnp
from jax import lax
from jax.sharding import PartitionSpec as P

KERNEL = 1.0 / (8.0 * math.pi)
BLOB = 0.25


def with_halo(x, sides, width):
    for axis, dim in sides:
        peers, length = (lax.axis_size(axis), x.shape[dim])
        up = [(i, (i + 1) % peers) for i in range(peers - 1)]
        down = [(j, i) for i, j in up]
        last = lax.slice_in_dim(x, length - width, length, axis=dim)
        first = lax.slice_in_dim(x, 0, width, axis=dim)
        before = lax.ppermute(last, axis, up)
        after = lax.ppermute(first, axis, down)
        x = jnp.concatenate([before, x, after], axis=dim)
    return x


def passed_along(x, axis, by):
    peers = lax.axis_size(axis)
    pairs = [(i, i + by) for i in range(peers) if 0 <= i + by < peers]
    return lax.ppermute(x, axis, pairs)


def pair_terms(target, source):
    xt = target[:, :3]
    ft = target[:, 3:]
    xs = source[:, :3]
    fs = source[:, 3:]
    sep = xt[:, :, :, None] - xs[:, :, None, :]
    rho_sq = jnp.sum(sep * sep, axis=1) + BLOB
    inv_one = lax.rsqrt(rho_sq)
    inv_three = inv_one / rho_sq
    inv_five = inv_three / rho_sq
    fa = ft[:, :, :, None]
    fb = fs[:, :, None, :]
    prod_ab = jnp.sum(fa * fb, axis=1)
    prod_ar = jnp.sum(fa * sep, axis=1)
    prod_br = jnp.sum(fb * sep, axis=1)
    first = (fa * prod_br[:, None] + fb * prod_ar[:, None] - prod_ab[:, None] * sep) * inv_three[
        :, None
    ]
    second = 3.0 * (prod_ar * prod_br * inv_five)[:, None] * sep
    return (first - second) * KERNEL


def one_hot(indices, count, dtype):
    return (indices[:, None] == jnp.arange(count, dtype=jnp.int32)[None, :]).astype(dtype)


def select_rows(indices, data):
    flat = data.reshape(data.shape[0], -1)
    picked = jnp.dot(
        one_hot(indices, data.shape[0], jnp.float32), flat, precision=lax.Precision.HIGHEST
    )
    return picked.reshape((indices.shape[0],) + data.shape[1:])


def add_rows(total, indices, values):
    hot = one_hot(indices, total.shape[0], jnp.float32)
    flat = values.reshape(values.shape[0], -1)
    added = jnp.dot(hot.T, flat, precision=lax.Precision.HIGHEST)
    return total + added.reshape(total.shape)


def per_device(
    positions,
    densities,
    near_src,
    near_count,
    far_slot,
    far_class,
    far_count,
    requests,
    up_basis,
    transfer_table,
    down_basis,
):
    leaf_num = near_count.shape[0]
    per_leaf = positions.shape[1] // leaf_num
    width = up_basis.shape[1]
    slot_num = near_src.shape[1]
    far_num = far_slot.shape[1]
    device = lax.axis_index("patch")
    stacked = jnp.concatenate([positions, densities], 0)
    window = with_halo(stacked, (("patch", 1),), stacked.shape[1])
    window = window.reshape(6, 3 * leaf_num, per_leaf).transpose(1, 0, 2)
    local = stacked.reshape(6, leaf_num, per_leaf).transpose(1, 0, 2)
    offset = (device - 1) * leaf_num
    start_state = (
        jnp.zeros((leaf_num, 3, per_leaf), jnp.float32),
        jnp.zeros((3 * leaf_num, 3, per_leaf), jnp.float32),
    )

    def near_step(slot, carry):
        tgt_sum, src_part = carry
        index = near_src[:, slot] - offset
        live = (slot < near_count).astype(jnp.float32)
        terms = pair_terms(local, select_rows(index, window)) * live[:, None, None, None]
        tgt_sum = tgt_sum + jnp.sum(terms, axis=3)
        src_part = add_rows(src_part, index, -jnp.sum(terms, axis=2))
        return (tgt_sum, src_part)

    tgt_sum, src_part = lax.fori_loop(0, slot_num, near_step, start_state)
    near = tgt_sum + src_part[leaf_num : 2 * leaf_num]
    for step_by, piece in ((-1, src_part[:leaf_num]), (1, src_part[2 * leaf_num :])):
        near = near + passed_along(piece, "patch", step_by)
    dens_leaf = local[:, 3:]
    dens_round = dens_leaf.reshape(leaf_num, 3 * per_leaf).astype(jnp.bfloat16)
    moments = jnp.einsum(
        "lrq,lq->lr", up_basis, dens_round, preferred_element_type=jnp.float32
    ).astype(jnp.bfloat16)
    asked = lax.all_to_all(requests[0], "patch", split_axis=0, concat_axis=0, tiled=True)
    replies = moments[asked].reshape(asked.shape[0], asked.shape[1] * width)
    table = lax.all_to_all(replies, "patch", split_axis=0, concat_axis=0, tiled=True).reshape(
        -1, width
    )
    operators = jnp.take(transfer_table, far_class.reshape(-1), axis=0).reshape(
        leaf_num, far_num, width, width
    )
    live_far = (jnp.arange(far_num, dtype=jnp.int32)[None, :] < far_count[:, None]).astype(
        jnp.bfloat16
    )
    sources = (
        jnp.take(table, far_slot.reshape(-1), axis=0).reshape(leaf_num, far_num, width)
        * live_far[:, :, None]
    )
    expansion = jnp.einsum("lsij,lsj->li", operators, sources, preferred_element_type=jnp.float32)
    expansion = expansion.astype(jnp.bfloat16)
    field = jnp.einsum("lr,lrqp->lqp", expansion, down_basis, preferred_element_type=jnp.float32)
    far = jnp.einsum(
        "lcp,lckp->lkp",
        dens_leaf,
        field.reshape(leaf_num, 3, 3, per_leaf),
        precision=lax.Precision.HIGHEST,
    )
    return (near + far).transpose(1, 0, 2).reshape(3, leaf_num * per_leaf)


def solution(mesh):
    placed = (
        P(None, "patch"),
        P(None, "patch"),
        P("patch", None),
        P("patch"),
        P("patch", None),
        P("patch", None),
        P("patch"),
        P("patch", None, None),
        P("patch", None, None),
        P(),
        P("patch", None, None, None),
    )
    return jax.shard_map(
        per_device, mesh=mesh, in_specs=placed, out_specs=P(None, "patch"), check_vma=False
    )
```

profile of v0, /device:TPU:8, one launch (start us, length us, event | category | flops | bytes accessed | tf_op | source)
XLA Modules:
  0.0 239.8 jit_solution(7807876388520252501)
XLA Ops:
  0.9 7.5 %collective-permute-start.1 = (f32[6,2048]{1,0:T(8,128)S(1)}, f32[6,2048]{1,0:T(8,128)S(1)}, u32[]{:S(2)}, u32[]{:S(2)}) collective-permute-start(f32[6,2048]{1,0:T(8,128)S(1)} %get-tuple-element.204), channel_id=1, source_target_pairs={{1,0},{2,1},{3,2},{4,3},{5,4},{6,5},{7,6},{8,7},{9,8},{10,9},{11,1... | collective-permute-start | bytes 147464 | tf_op jit(solution)/shard_map/ppermute | solution.py:20
  11.7 10.0 %all-to-all-start = ((s32[128,1,4]{2,1,0:T(1,128)}), s32[128,1,4]{2,1,0:T(1,128)S(1)}, u32[]{:S(2)}, u32[]{:S(2)}) async-start(s32[128,1,4]{2,1,0:T(1,128)} %bitcast.9), calls=%async_computation | async-start | bytes 131072 | tf_op jit(solution)/shard_map/all_to_all | solution.py:119
  25.6 40.8 %gather_fusion = bf16[512,20736]{1,0:T(8,128)(2,1)} fusion(bf16[189,20736]{1,0:T(8,128)(2,1)} %param.22, s32[1024]{0:T(1024)S(1)} %pad_clamp_fusion.2), kind=kCustom, calls=%fused_computation | custom fusion | bytes 42469376 | tf_op jit(solution)/shard_map/jit(_take)/gather | solution.py:124
  66.4 67.3 %gather.16 = bf16[16,32,144,144]{3,2,1,0:T(8,128)(2,1)} reshape(bf16[512,20736]{1,0:T(8,128)(2,1)} %gather_fusion) | data formatting | bytes 42467328 | tf_op jit(solution)/shard_map/jit(_take)/gather | solution.py:124
  139.3 9.8 %all-to-all-start.1 = ((bf16[128,2,288]{2,1,0:T(2,128)(2,1)}), bf16[128,2,288]{2,1,0:T(2,128)(2,1)S(1)}, u32[]{:S(2)}, u32[]{:S(2)}) async-start(bf16[128,2,288]{2,1,0:T(2,128)(2,1)} %reshape.271), calls=%async_computation.1 | async-start | bytes 393216 | tf_op jit(solution)/shard_map/all_to_all | solution.py:121
  149.2 56.9 %while.16 = (s32[]{:T(128)}, f32[16,3,128]{2,1,0:T(4,128)S(1)}, f32[48,3,128]{2,0,1:T(8,128)S(1)}, f32[16,6,128]{2,1,0:T(8,128)S(1)}, s32[16,8]{0,1:T(8,128)}, /...) while((s32[]{:T(128)}, f32[16,3,128]{2,1,0:T(4,128)S(1)}, ...), condition=%wide.region_7.0_spmd.clone, body=%wide.region_0.0_spmd.clone.sunk | while | flops 27962928 | bytes 15712836 | solution.py:110
  150.2 2.2 fusion.58
  152.9 3.0 %fusion.59 = (f32[16,3,128]{2,1,0:T(4,128)S(1)}, f32[16,3,128]{2,1,0:T(4,128)S(1)}) fusion(f32[16]{0:T(128)S(1)} %compare_select_fusion.7, f32[16,128,128]{2,1,0:T(8,128)S(1)} %get-tuple-element.276, f32[16,128,128]{2,1,0:T(8,128)S(1)} %get-tuple-element.277, f32[16,128,128]{2,1,0:T(8,128)S(1)} %get-tuple-element.278, ...), kind=kLoop, calls=%fused_computation.16.clone.1 | loop fusion | flops 9424896 | bytes 5390400 | tf_op jit(solution)/shard_map/while/body/eval_jaxpr/reduce_sum | solution.py:107
  157.3 2.2 fusion.58
  160.0 3.0 %fusion.59 = (f32[16,3,128]{2,1,0:T(4,128)S(1)}, f32[16,3,128]{2,1,0:T(4,128)S(1)}) fusion(f32[16]{0:T(128)S(1)} %compare_select_fusion.7, f32[16,128,128]{2,1,0:T(8,128)S(1)} %get-tuple-element.276, f32[16,128,128]{2,1,0:T(8,128)S(1)} %get-tuple-element.277, f32[16,128,128]{2,1,0:T(8,128)S(1)} %get-tuple-element.278, ...), kind=kLoop, calls=%fused_computation.16.clone.1 | loop fusion | flops 9424896 | bytes 5390400 | tf_op jit(solution)/shard_map/while/body/eval_jaxpr/reduce_sum | solution.py:107
  164.4 2.2 fusion.58
  167.1 3.0 %fusion.59 = (f32[16,3,128]{2,1,0:T(4,128)S(1)}, f32[16,3,128]{2,1,0:T(4,128)S(1)}) fusion(f32[16]{0:T(128)S(1)} %compare_select_fusion.7, f32[16,128,128]{2,1,0:T(8,128)S(1)} %get-tuple-element.276, f32[16,128,128]{2,1,0:T(8,128)S(1)} %get-tuple-element.277, f32[16,128,128]{2,1,0:T(8,128)S(1)} %get-tuple-element.278, ...), kind=kLoop, calls=%fused_computation.16.clone.1 | loop fusion | flops 9424896 | bytes 5390400 | tf_op jit(solution)/shard_map/while/body/eval_jaxpr/reduce_sum | solution.py:107
  171.6 2.2 fusion.58
  174.2 3.0 %fusion.59 = (f32[16,3,128]{2,1,0:T(4,128)S(1)}, f32[16,3,128]{2,1,0:T(4,128)S(1)}) fusion(f32[16]{0:T(128)S(1)} %compare_select_fusion.7, f32[16,128,128]{2,1,0:T(8,128)S(1)} %get-tuple-element.276, f32[16,128,128]{2,1,0:T(8,128)S(1)} %get-tuple-element.277, f32[16,128,128]{2,1,0:T(8,128)S(1)} %get-tuple-element.278, ...), kind=kLoop, calls=%fused_computation.16.clone.1 | loop fusion | flops 9424896 | bytes 5390400 | tf_op jit(solution)/shard_map/while/body/eval_jaxpr/reduce_sum | solution.py:107
  178.7 2.2 fusion.58
  181.4 3.0 %fusion.59 = (f32[16,3,128]{2,1,0:T(4,128)S(1)}, f32[16,3,128]{2,1,0:T(4,128)S(1)}) fusion(f32[16]{0:T(128)S(1)} %compare_select_fusion.7, f32[16,128,128]{2,1,0:T(8,128)S(1)} %get-tuple-element.276, f32[16,128,128]{2,1,0:T(8,128)S(1)} %get-tuple-element.277, f32[16,128,128]{2,1,0:T(8,128)S(1)} %get-tuple-element.278, ...), kind=kLoop, calls=%fused_computation.16.clone.1 | loop fusion | flops 9424896 | bytes 5390400 | tf_op jit(solution)/shard_map/while/body/eval_jaxpr/reduce_sum | solution.py:107
  185.8 2.2 fusion.58
  188.5 3.0 %fusion.59 = (f32[16,3,128]{2,1,0:T(4,128)S(1)}, f32[16,3,128]{2,1,0:T(4,128)S(1)}) fusion(f32[16]{0:T(128)S(1)} %compare_select_fusion.7, f32[16,128,128]{2,1,0:T(8,128)S(1)} %get-tuple-element.276, f32[16,128,128]{2,1,0:T(8,128)S(1)} %get-tuple-element.277, f32[16,128,128]{2,1,0:T(8,128)S(1)} %get-tuple-element.278, ...), kind=kLoop, calls=%fused_computation.16.clone.1 | loop fusion | flops 9424896 | bytes 5390400 | tf_op jit(solution)/shard_map/while/body/eval_jaxpr/reduce_sum | solution.py:107
  192.9 2.2 fusion.58
  195.6 3.0 %fusion.59 = (f32[16,3,128]{2,1,0:T(4,128)S(1)}, f32[16,3,128]{2,1,0:T(4,128)S(1)}) fusion(f32[16]{0:T(128)S(1)} %compare_select_fusion.7, f32[16,128,128]{2,1,0:T(8,128)S(1)} %get-tuple-element.276, f32[16,128,128]{2,1,0:T(8,128)S(1)} %get-tuple-element.277, f32[16,128,128]{2,1,0:T(8,128)S(1)} %get-tuple-element.278, ...), kind=kLoop, calls=%fused_computation.16.clone.1 | loop fusion | flops 9424896 | bytes 5390400 | tf_op jit(solution)/shard_map/while/body/eval_jaxpr/reduce_sum | solution.py:107
  202.7 3.0 %fusion.59 = (f32[16,3,128]{2,1,0:T(4,128)S(1)}, f32[16,3,128]{2,1,0:T(4,128)S(1)}) fusion(f32[16]{0:T(128)S(1)} %compare_select_fusion.7, f32[16,128,128]{2,1,0:T(8,128)S(1)} %get-tuple-element.276, f32[16,128,128]{2,1,0:T(8,128)S(1)} %get-tuple-element.277, f32[16,128,128]{2,1,0:T(8,128)S(1)} %get-tuple-element.278, ...), kind=kLoop, calls=%fused_computation.16.clone.1 | loop fusion | flops 9424896 | bytes 5390400 | tf_op jit(solution)/shard_map/while/body/eval_jaxpr/reduce_sum | solution.py:107
  208.2 7.8 %collective-permute-start.2 = (f32[16,3,128]{2,0,1:T(8,128)S(1)}, f32[16,3,128]{2,0,1:T(8,128)S(1)}, u32[]{:S(2)}, u32[]{:S(2)}) collective-permute-start(f32[16,3,128]{2,0,1:T(8,128)S(1)} %get-tuple-element.202), channel_id=1, source_target_pairs={{1,0},{2,1},{3,2},{4,3},{5,4},{6,5},{7,6},{8,7},{9,8},{10,9},{11,1... | collective-permute-start | bytes 73736 | tf_op jit(solution)/shard_map/ppermute | solution.py:28
  219.9 15.8 %fusion.21 = bf16[16,1,144,1]{2,1,3,0:T(2,128)(2,1)S(1)} fusion(bf16[16,32,144,144]{3,2,1,0:T(8,128)(2,1)} %gather.16, pred[16,32]{1,0:T(8,128)(4,1)S(1)} %compare_and_fusion.1, bf16[16,32,144,1]{2,1,0,3:T(8,128)(2,1)S(1)} %multiply_bitcast_fusion), kind=kOutput, calls=%fused_computation.37 | convolution fusion | flops 31850496 | bytes 21386240 | tf_op jit(solution)/shard_map/lsij,lsj->li/dot_general | solution.py:134
  235.7 3.4 %fusion.29 = f32[16,1,9,128]{3,1,2,0:T(1,128)S(1)} fusion(bf16[16,144,9,128]{3,1,2,0:T(8,128)(2,1)} %param.23, bf16[16,144,1,1]{1,0,2,3:T(8,128)(2,1)S(1)} %bitcast.109), kind=kOutput, calls=%fused_computation.59 | convolution fusion | flops 5308416 | bytes 5386752 | tf_op jit(solution)/shard_map/lr,lrqp->lqp/dot_general | solution.py:136
  (145 shorter events, 36.5 us)
Async XLA Ops:
  0.0 24.9 %copy-start = (bf16[16,144,384]{2,1,0:T(8,128)(2,1)S(1)}, bf16[16,144,384]{2,1,0:T(8,128)(2,1)}, u32[]{:S(2)}) copy-start(bf16[16,144,384]{2,1,0:T(8,128)(2,1)} %param.21) | copy-start | bytes 5308420
  0.9 148.2 %collective-permute-start.1 = (f32[6,2048]{1,0:T(8,128)S(1)}, f32[6,2048]{1,0:T(8,128)S(1)}, u32[]{:S(2)}, u32[]{:S(2)}) collective-permute-start(f32[6,2048]{1,0:T(8,128)S(1)} %get-tuple-element.204), channel_id=1, source_target_pairs={{1,0},{2,1},{3,2},{4,3},{5,4},{6,5},{7,6},{8,7},{9,8},{10,9},{11,1... | collective-permute-start | bytes 147464 | tf_op jit(solution)/shard_map/ppermute | solution.py:20
  8.4 140.7 %collective-permute-start = (f32[6,2048]{1,0:T(8,128)S(1)}, f32[6,2048]{1,0:T(8,128)S(1)}, u32[]{:S(2)}, u32[]{:S(2)}) collective-permute-start(f32[6,2048]{1,0:T(8,128)S(1)} %get-tuple-element.204), channel_id=1, source_target_pairs={{0,1},{1,2},{2,3},{3,4},{4,5},{5,6},{6,7},{7,8},{8,9},{9,10},{10,1... | collective-permute-start | bytes 147464 | tf_op jit(solution)/shard_map/ppermute | solution.py:19
  11.7 122.0 %all-to-all-start = ((s32[128,1,4]{2,1,0:T(1,128)}), s32[128,1,4]{2,1,0:T(1,128)S(1)}, u32[]{:S(2)}, u32[]{:S(2)}) async-start(s32[128,1,4]{2,1,0:T(1,128)} %bitcast.9), calls=%async_computation | async-start | bytes 131072 | tf_op jit(solution)/shard_map/all_to_all | solution.py:119
  133.7 15.4 %copy-start.2 = (f32[3,2048]{1,0:T(4,128)S(1)}, f32[3,2048]{1,0:T(4,128)}, u32[]{:S(2)}) copy-start(f32[3,2048]{1,0:T(4,128)} %param.14) | copy-start | bytes 73732
  133.7 15.4 %copy-start.3 = (f32[3,2048]{1,0:T(4,128)S(1)}, f32[3,2048]{1,0:T(4,128)}, u32[]{:S(2)}) copy-start(f32[3,2048]{1,0:T(4,128)} %param.13) | copy-start | bytes 73732
  133.7 15.5 %copy-start.4 = (s32[16]{0:T(128)S(1)}, s32[16]{0:T(128)}, u32[]{:S(2)}) copy-start(s32[16]{0:T(128)} %param.16) | copy-start | bytes 196
  139.3 76.6 %all-to-all-start.1 = ((bf16[128,2,288]{2,1,0:T(2,128)(2,1)}), bf16[128,2,288]{2,1,0:T(2,128)(2,1)S(1)}, u32[]{:S(2)}, u32[]{:S(2)}) async-start(bf16[128,2,288]{2,1,0:T(2,128)(2,1)} %reshape.271), calls=%async_computation.1 | async-start | bytes 393216 | tf_op jit(solution)/shard_map/all_to_all | solution.py:121
  206.1 33.0 %collective-permute-start.3 = (f32[16,3,128]{2,0,1:T(8,128)S(1)}, f32[16,3,128]{2,0,1:T(8,128)S(1)}, u32[]{:S(2)}, u32[]{:S(2)}) collective-permute-start(f32[16,3,128]{2,0,1:T(8,128)S(1)} %get-tuple-element.203), channel_id=1, source_target_pairs={{0,1},{1,2},{2,3},{3,4},{4,5},{5,6},{6,7},{7,8},{8,9},{9,10},{10,1... | collective-permute-start | bytes 73736 | tf_op jit(solution)/shard_map/ppermute | solution.py:28
  208.2 31.0 %collective-permute-start.2 = (f32[16,3,128]{2,0,1:T(8,128)S(1)}, f32[16,3,128]{2,0,1:T(8,128)S(1)}, u32[]{:S(2)}, u32[]{:S(2)}) collective-permute-start(f32[16,3,128]{2,0,1:T(8,128)S(1)} %get-tuple-element.202), channel_id=1, source_target_pairs={{1,0},{2,1},{3,2},{4,3},{5,4},{6,5},{7,6},{8,7},{9,8},{10,9},{11,1... | collective-permute-start | bytes 73736 | tf_op jit(solution)/shard_map/ppermute | solution.py:28
  219.9 19.9 %copy-start.1 = (bf16[16,144,384]{2,1,0:T(8,128)(2,1)S(1)}, bf16[16,144,384]{2,1,0:T(8,128)(2,1)}, u32[]{:S(2)}) copy-start(bf16[16,144,384]{2,1,0:T(8,128)(2,1)} %param.21) | copy-start | bytes 5308420
where the time goes:
time: 241 us; the launch traced here: 240 us
  local copies, waits for them, and re-layouts  119 us (49%)
  other arithmetic  56.9 us (24%)
  starting transfers between devices  38.9 us (16%)
  matrix products  24 us (10%)
    gather x2, local copies, waits for them, and re-layouts, per_device(): jnp.take(transfer_table, far_class.reshape(-1), axis=0)  108 us
    reduce_sum x8, other arithmetic, near_step(): src_part = add_rows(src_part, index, -jnp.sum(terms, axis=2))  24.2 us
    reduce_sum x8, other arithmetic, pair_terms(): rho_sq = jnp.sum(sep * sep, axis=1) + BLOB  18 us
    dot_general x1, matrix products, per_device(): jnp.einsum('lsij,lsj->li', operators, sources, preferred_element_type=jnp...  15.8 us
    all_to_all x1, starting transfers between devices, per_device(): lax.all_to_all(requests[0], 'patch', split_axis=0, concat_axis=0, tiled=T...  10 us
    ppermute x2, starting transfers between devices, passed_along(): return lax.ppermute(x, axis, pairs)  9.78 us
    all_to_all x1, starting transfers between devices, per_device(): lax.all_to_all(replies, 'patch', split_axis=0, concat_axis=0, tiled=True)  9.76 us
    ppermute x1, starting transfers between devices, with_halo(): after = lax.ppermute(first, axis, down)  7.47 us
  transfers between devices with their start and end apart: 6, of which 0 were waited for; matrix products, arithmetic and copies ran while one was open for 82% of the time, Pallas kernels for 0%

commit v1 on v0

v1 whole, which is shorter than its diff:
```python
import math

import jax
import jax.numpy as jnp
import numpy as np
from jax import lax
from jax.experimental import pallas as pl
from jax.experimental.pallas import tpu as pltpu
from jax.sharding import PartitionSpec as P

KERNEL = 1.0 / (8.0 * math.pi)
BLOB = 0.25
PITCH = 9
F32 = jnp.float32
BF16 = jnp.bfloat16


def with_halo(x, sides, width):
    for axis, dim in sides:
        peers, length = (lax.axis_size(axis), x.shape[dim])
        up = [(i, (i + 1) % peers) for i in range(peers - 1)]
        down = [(j, i) for i, j in up]
        last = lax.slice_in_dim(x, length - width, length, axis=dim)
        first = lax.slice_in_dim(x, 0, width, axis=dim)
        before = lax.ppermute(last, axis, up)
        after = lax.ppermute(first, axis, down)
        x = jnp.concatenate([before, x, after], axis=dim)
    return x


def passed_along(x, axis, by):
    peers = lax.axis_size(axis)
    pairs = [(i, i + by) for i in range(peers) if 0 <= i + by < peers]
    return lax.ppermute(x, axis, pairs)


def near_kernel(idx_ref, cnt_ref, win_ref, tgt_ref, src_ref, cols, racc, sacc):
    leaves = tgt_ref.shape[0]
    tiles = racc.shape[1] // 8
    sacc[...] = jnp.zeros_like(sacc)

    def leaf_step(leaf, _):
        turned = jnp.transpose(win_ref[leaves + leaf], (1, 0))
        for k in range(6):
            cols[k] = jnp.broadcast_to(turned[:, k : k + 1], cols.shape[1:])
        racc[...] = jnp.zeros_like(racc)

        def slot_step(slot, _):
            other = idx_ref[leaf * 8 + slot]
            source = win_ref[other]
            rows = [jnp.broadcast_to(source[k : k + 1], (8, 128)) for k in range(6)]
            xs, fs = rows[:3], rows[3:]
            down = [jnp.zeros((8, 128), F32) for _ in range(3)]
            for tile in range(tiles):
                part = pl.ds(8 * tile, 8)
                fa = [cols[3 + k, part] for k in range(3)]
                sep = [cols[k, part] - xs[k] for k in range(3)]
                rho = (sep[0] * sep[0] + sep[1] * sep[1]) + (sep[2] * sep[2] + BLOB)
                inv = lax.rsqrt(rho)
                inv_two = inv * inv
                inv_three = inv_two * inv
                ab = fa[0] * fs[0] + fa[1] * fs[1] + fa[2] * fs[2]
                ar = fa[0] * sep[0] + fa[1] * sep[1] + fa[2] * sep[2]
                br = fs[0] * sep[0] + fs[1] * sep[1] + fs[2] * sep[2]
                on_b = ar * inv_three
                on_a = br * inv_three
                on_r = ab * inv_three + (on_b * br) * (inv_two * 3.0)
                for k in range(3):
                    term = fa[k] * on_a + fs[k] * on_b - on_r * sep[k]
                    racc[k, part] += term
                    down[k] = down[k] + term
            for k in range(3):
                sacc[other, k] -= down[k]
            return 0

        lax.fori_loop(0, cnt_ref[leaf], slot_step, 0)
        for k in range(3):
            turned = jnp.transpose(racc[k], (1, 0))
            tgt_ref[leaf, k : k + 1] = jnp.sum(turned, axis=0, keepdims=True) * KERNEL
        return 0

    lax.fori_loop(0, leaves, leaf_step, 0)

    def out_step(leaf, _):
        for k in range(3):
            src_ref[leaf, k : k + 1] = jnp.sum(sacc[leaf, k], axis=0, keepdims=True) * KERNEL
        return 0

    lax.fori_loop(0, src_ref.shape[0], out_step, 0)


def near_call(index, count, window):
    leaves = count.shape[0]
    smem = pl.BlockSpec(memory_space=pltpu.SMEM)
    vmem = pl.BlockSpec(memory_space=pltpu.VMEM)
    return pl.pallas_call(
        near_kernel,
        name="near",
        out_shape=(
            jax.ShapeDtypeStruct((leaves, 3, 128), F32),
            jax.ShapeDtypeStruct((3 * leaves, 3, 128), F32),
        ),
        in_specs=[smem, smem, vmem],
        out_specs=(vmem, vmem),
        scratch_shapes=[
            pltpu.VMEM((6, 128, 128), F32),
            pltpu.VMEM((3, 128, 128), F32),
            pltpu.VMEM((3 * leaves, 3, 8, 128), F32),
        ],
        compiler_params=pltpu.CompilerParams(vmem_limit_bytes=16 << 20),
        cost_estimate=pl.CostEstimate(flops=10**8, bytes_accessed=10**6, transcendentals=10**6),
    )(index, count, window)


def far_kernel(
    slot_ref,
    class_ref,
    cnt_ref,
    mom_ref,
    sel_ref,
    seg_ref,
    rep_ref,
    dens_ref,
    table_hbm,
    basis_hbm,
    out_ref,
    table,
    wide,
    basis,
    pattern,
    sums,
    splat,
    sems,
):
    leaves = out_ref.shape[0]
    classes = table_hbm.shape[0]
    chunks = table_hbm.shape[1] // 128
    get_table = pltpu.make_async_copy(table_hbm, table, sems.at[0])
    get_basis = pltpu.make_async_copy(basis_hbm, basis, sems.at[1])
    get_table.start()
    get_basis.start()
    for v in range(9):
        part = sel_ref[:, 128 * v : 128 * v + 128]
        pattern[v] = jnp.dot(mom_ref[...], part, preferred_element_type=F32)
    get_table.wait()

    def widen(block, _):
        def piece(step, _):
            for sub in range(9):
                chunk = step * 9 + sub
                lanes = pl.ds(pl.multiple_of(chunk * 128, 128), 128)
                rows = pl.ds(pl.multiple_of(block * 8, 8), 8)
                wide[pl.ds((block * chunks + chunk) * PITCH, 8)] = table[rows, lanes].astype(F32)
            return 0

        lax.fori_loop(0, chunks // 9, piece, 0)
        return 0

    full = classes // 8
    lax.fori_loop(0, full, widen, 0)

    def tail(step, _):
        for sub in range(9):
            chunk = step * 9 + sub
            lanes = pl.ds(pl.multiple_of(chunk * 128, 128), 128)
            wide[pl.ds((full * chunks + chunk) * PITCH, classes - 8 * full)] = table[
                8 * full :, lanes
            ].astype(F32)
        return 0

    lax.fori_loop(0, chunks // 9, tail, 0)

    def leaf_step(leaf, _):
        def slot_step(slot, acc):
            kind = class_ref[leaf * 32 + slot]
            place = slot_ref[leaf * 32 + slot]
            base = (kind // 8) * (chunks * PITCH) + kind % 8
            new = []
            for v in range(9):
                p = jnp.broadcast_to(pattern[v, pl.ds(place, 1), :], (8, 128))
                for g in range(3):
                    t = wide[pl.ds(base + (72 * g + v) * PITCH, 8, stride=9 * PITCH), :]
                    new.append(acc[3 * v + g] + p * t)
            return tuple(new)

        zero = jnp.zeros((8, 128), F32)
        acc = lax.fori_loop(0, cnt_ref[leaf], slot_step, (zero,) * 27)
        for v in range(9):
            for g in range(3):
                rows = pl.ds(pl.multiple_of(leaf * 24 + 8 * g, 8), 8)
                sums[rows, pl.ds(128 * v, 128)] = acc[3 * v + g]
        return 0

    lax.fori_loop(0, leaves, leaf_step, 0)
    total = sums[...]
    high = total.astype(BF16)
    low = (total - high.astype(F32)).astype(BF16)
    expansion = jnp.dot(high, seg_ref[...], preferred_element_type=F32) + jnp.dot(
        low, seg_ref[...], preferred_element_type=F32
    )
    expansion = expansion.astype(BF16)
    for w in range(8):
        part = rep_ref[:, 128 * w : 128 * w + 128]
        splat[w] = jnp.dot(expansion, part, preferred_element_type=F32)
    get_basis.wait()

    def down_step(leaf, _):
        def group(u, acc):
            acc = list(acc)
            for w in range(8):
                x = jnp.broadcast_to(splat[w, pl.ds(leaf * 24 + u, 1), :], (8, 128))
                d = basis[leaf, u * 8 + w].astype(F32)
                top, last = acc[w % 2]
                acc[w % 2] = (top + x * d[:8], last + x[:1] * d[8:])
            return tuple(acc)

        zero = (jnp.zeros((8, 128), F32), jnp.zeros((1, 128), F32))
        acc = lax.fori_loop(0, 18, group, (zero, zero))
        top = acc[0][0] + acc[1][0]
        last = acc[0][1] + acc[1][1]
        f = dens_ref[leaf]
        out_ref[leaf] = (
            f[0:1] * top[0:3]
            + f[1:2] * top[3:6]
            + f[2:3] * jnp.concatenate([top[6:8], last], axis=0)
        )
        return 0

    lax.fori_loop(0, leaves, down_step, 0)


def far_consts(width):
    flat = np.arange(9 * 128)
    sel = (flat[None, :] % width == np.arange(width)[:, None]).astype(np.float32)
    seg = (flat[:, None] // width == np.arange(128)[None, :]).astype(np.float32)
    rep = (np.arange(1024)[None, :] // 128 == np.arange(128)[:, None]).astype(np.float32)
    return [jnp.asarray(m, BF16) for m in (sel, seg, rep)]


def far_call(slots, kinds, count, moments, dens, table, basis):
    leaves = count.shape[0]
    width = basis.shape[1]
    classes = table.shape[0]
    chunks = table.shape[1] // 128
    blocks = -(-classes // 8)
    sel, seg, rep = far_consts(width)
    smem = pl.BlockSpec(memory_space=pltpu.SMEM)
    vmem = pl.BlockSpec(memory_space=pltpu.VMEM)
    hbm = pl.BlockSpec(memory_space=pltpu.HBM)
    return pl.pallas_call(
        far_kernel,
        name="far",
        out_shape=jax.ShapeDtypeStruct((leaves, 3, 128), F32),
        in_specs=[smem] * 3 + [vmem] * 5 + [hbm, hbm],
        out_specs=vmem,
        scratch_shapes=[
            pltpu.VMEM(table.shape, BF16),
            pltpu.VMEM(((blocks * chunks + 54) * PITCH, 128), F32),
            pltpu.VMEM(basis.shape, BF16),
            pltpu.VMEM((9, moments.shape[0], 128), F32),
            pltpu.VMEM((leaves * 24, 1152), F32),
            pltpu.VMEM((8, leaves * 24, 128), F32),
            pltpu.SemaphoreType.DMA((2,)),
        ],
        compiler_params=pltpu.CompilerParams(vmem_limit_bytes=56 << 20),
        cost_estimate=pl.CostEstimate(flops=10**8, bytes_accessed=2 * 10**7, transcendentals=0),
    )(slots, kinds, count, moments, sel, seg, rep, dens, table, basis)


def per_device(
    positions,
    densities,
    near_src,
    near_count,
    far_slot,
    far_class,
    far_count,
    requests,
    up_basis,
    transfer_table,
    down_basis,
):
    leaf_num = near_count.shape[0]
    per_leaf = positions.shape[1] // leaf_num
    width = up_basis.shape[1]
    device = lax.axis_index("patch")
    stacked = jnp.concatenate([positions, densities], 0)
    window = with_halo(stacked, (("patch", 1),), stacked.shape[1])
    window = window.reshape(6, 3 * leaf_num, per_leaf).transpose(1, 0, 2)
    window = jnp.pad(window, ((0, 0), (0, 2), (0, 0)))
    local = stacked.reshape(6, leaf_num, per_leaf).transpose(1, 0, 2)
    offset = (device - 1) * leaf_num
    tgt_sum, src_part = near_call((near_src - offset).reshape(-1), near_count, window)
    near = tgt_sum + src_part[leaf_num : 2 * leaf_num]
    for step_by, piece in ((-1, src_part[:leaf_num]), (1, src_part[2 * leaf_num :])):
        near = near + passed_along(piece, "patch", step_by)
    dens_leaf = local[:, 3:]
    dens_round = dens_leaf.reshape(leaf_num, 3 * per_leaf).astype(BF16)
    moments = jnp.einsum("lrq,lq->lr", up_basis, dens_round, preferred_element_type=F32).astype(BF16)
    asked = lax.all_to_all(requests[0], "patch", split_axis=0, concat_axis=0, tiled=True)
    replies = moments[asked].reshape(asked.shape[0], asked.shape[1] * width)
    table = lax.all_to_all(replies, "patch", split_axis=0, concat_axis=0, tiled=True).reshape(
        -1, width
    )
    far = far_call(
        far_slot.reshape(-1),
        far_class.reshape(-1),
        far_count,
        table,
        dens_leaf,
        transfer_table,
        down_basis,
    )
    return (near + far).transpose(1, 0, 2).reshape(3, leaf_num * per_leaf)


def solution(mesh):
    placed = (
        P(None, "patch"),
        P(None, "patch"),
        P("patch", None),
        P("patch"),
        P("patch", None),
        P("patch", None),
        P("patch"),
        P("patch", None, None),
        P("patch", None, None),
        P(),
        P("patch", None, None, None),
    )
    return jax.shard_map(
        per_device, mesh=mesh, in_specs=placed, out_specs=P(None, "patch"), check_vma=False
    )
```

time: 241 us -> 108 us (0.45)
  local copies, waits for them, and re-layouts: 119 us -> 17.3 us
  other arithmetic: 56.9 us -> 5.06 us
  Pallas kernels: 0 us -> 39.2 us
  matrix products: 24 us -> 0.69 us
  waiting for transfers between devices: 0.02 us -> 8.01 us
    gather x3 -> x0, local copies, waits for them, and re-layouts: 110 us -> none  [the longest x2 108 us: per_device(): jnp.take(transfer_table, far_class.reshape(-1), axis=0)]
    reduce_sum x16 -> x0, other arithmetic: 42.2 us -> none  [the longest x8 24.2 us: near_step(): src_part = add_rows(src_part, index, -jnp.sum(terms, axis=2))]
    pallas_call x0 -> x2, Pallas kernels: none -> 39.2 us  [the longest x1 28.1 us: far_call(): pl.pallas_call(far_kernel, name='far', out_shape=jax.ShapeDtypeStruct((le...]
    dot_general x19 -> x1, matrix products: 24 us -> 0.69 us  [per_device(): jnp.einsum('lrq,lq->lr', up_basis, dens_round, preferred_element_type=F32)]
    all_to_all x1, waiting for transfers between devices: 0.01 us -> 8 us  [per_device(): lax.all_to_all(requests[0], 'patch', split_axis=0, concat_axis=0, tiled=T...]
    unnamed x17 -> x18, local copies, waits for them, and re-layouts: 3.23 us -> 11.2 us
    eq x8 -> x0, other arithmetic: 5.6 us -> none  [one_hot(): indices[:, None] == jnp.arange(count, dtype=jnp.int32)[None, :]]
    all_to_all x1, starting transfers between devices: 9.76 us -> 5.18 us  [per_device(): lax.all_to_all(replies, 'patch', split_axis=0, concat_axis=0, tiled=True)]
  transfers between devices with their start and end apart: 6 -> 6, of which waited for: 0 -> 1; matrix products, arithmetic and copies ran while one was open for 82% -> 19% of each run, Pallas kernels for 0% -> 37%
where the time goes in v1:
time: 108 us; the launch traced here: 107 us
  Pallas kernels  39.2 us (36%)
  starting transfers between devices  36.5 us (34%)
  local copies, waits for them, and re-layouts  17.3 us (16%)
  waiting for transfers between devices  8.01 us (7%)
  other arithmetic  5.06 us (5%)
    pallas_call x1, Pallas kernels, far_call(): pl.pallas_call(far_kernel, name='far', out_shape=jax.ShapeDtypeStruct((le...  28.1 us
    ppermute x2, starting transfers between devices, passed_along(): return lax.ppermute(x, axis, pairs)  11.9 us
    unnamed x18, local copies, waits for them, and re-layouts  11.2 us
    pallas_call x1, Pallas kernels, near_call(): pl.pallas_call(near_kernel, name='near', out_shape=(jax.ShapeDtypeStruct(...  11.1 us
    all_to_all x1, starting transfers between devices, per_device(): lax.all_to_all(requests[0], 'patch', split_axis=0, concat_axis=0, tiled=T...  10 us
    all_to_all x1, waiting for transfers between devices, per_device(): lax.all_to_all(requests[0], 'patch', split_axis=0, concat_axis=0, tiled=T...  8 us
    ppermute x1, starting transfers between devices, with_halo(): after = lax.ppermute(first, axis, down)  7.47 us
    all_to_all x1, starting transfers between devices, per_device(): lax.all_to_all(replies, 'patch', split_axis=0, concat_axis=0, tiled=True)  5.18 us
  transfers between devices with their start and end apart: 6, of which 1 were waited for; matrix products, arithmetic and copies ran while one was open for 19% of the time, Pallas kernels for 37%

profile of v1, /device:TPU:8, one launch (start us, length us, event | category | flops | bytes accessed | tf_op | source)
XLA Modules:
  0.0 107.0 jit_solution(5345656106244891392)
XLA Ops:
  0.0 0.9 pad_maximum_fusion
  0.9 7.5 %collective-permute-start.1 = (f32[6,2048]{1,0:T(8,128)S(1)}, f32[6,2048]{1,0:T(8,128)S(1)}, u32[]{:S(2)}, u32[]{:S(2)}) collective-permute-start(f32[6,2048]{1,0:T(8,128)S(1)} %get-tuple-element.11), channel_id=1, source_target_pairs={{1,0},{2,1},{3,2},{4,3},{5,4},{6,5},{7,6},{8,7},{9,8},{10,9},{11,1... | collective-permute-start | bytes 147464 | tf_op jit(solution)/shard_map/ppermute | solution.py:26
  8.4 1.9 %collective-permute-start = (f32[6,2048]{1,0:T(8,128)S(1)}, f32[6,2048]{1,0:T(8,128)S(1)}, u32[]{:S(2)}, u32[]{:S(2)}) collective-permute-start(f32[6,2048]{1,0:T(8,128)S(1)} %get-tuple-element.11), channel_id=1, source_target_pairs={{0,1},{1,2},{2,3},{3,4},{4,5},{5,6},{6,7},{7,8},{8,9},{9,10},{10,1... | collective-permute-start | bytes 147464 | tf_op jit(solution)/shard_map/ppermute | solution.py:25
  10.3 1.4 %copy.21 = s32[1,128,4]{2,1,0:T(8,128)} copy(s32[1,128,4]{1,2,0:T(4,128)} %param.21) | data formatting | bytes 4096 | tf_op args[7]
  11.8 10.0 %all-to-all-start = ((s32[128,1,4]{2,1,0:T(1,128)}), s32[128,1,4]{2,1,0:T(1,128)S(1)}, u32[]{:S(2)}, u32[]{:S(2)}) async-start(s32[128,1,4]{2,1,0:T(1,128)} %bitcast.5), calls=%async_computation | async-start | bytes 131072 | tf_op jit(solution)/shard_map/all_to_all | solution.py:300
  21.8 0.7 fusion.2
  22.7 8.0 %all-to-all-done = s32[128,1,4]{2,1,0:T(1,128)S(1)} async-done(((s32[128,1,4]{2,1,0:T(1,128)}), s32[128,1,4]{2,1,0:T(1,128)S(1)}, u32[]{:S(2)}, u32[]{:S(2)}) %all-to-all-start) | async-done | bytes 2080 | tf_op jit(solution)/shard_map/all_to_all | solution.py:300
  30.9 2.0 %gather_fusion = bf16[512,144]{1,0:T(8,128)(2,1)S(1)} fusion(bf16[16,144]{1,0:T(8,128)(2,1)S(1)} %bitcast.21, s32[1024]{0:T(1024)S(1)} %pad_clamp_fusion), kind=kCustom, calls=%fused_computation | custom fusion | bytes 296960 | tf_op jit(solution)/shard_map/gather | solution.py:301
  32.9 0.4 all_to_all.19
  33.3 0.5 broadcast.21
  33.8 1.7 %reduce.1 = bf16[128,576]{1,0:T(8,128)(2,1)S(1)} reduce(bf16[128,1,576]{2,1,0:T(2,128)(2,1)S(1)} %all_to_all.19, bf16[]{:T(256)} %broadcast.21), dimensions={1}, to_apply=%all_to_all.19.reduce_sub_computation | reduce | bytes 294914 | tf_op jit(solution)/shard_map/all_to_all | solution.py:302
  35.5 0.9 reshape.81
  36.4 5.2 %all-to-all-start.1 = ((bf16[128,2,288]{2,1,0:T(2,128)(2,1)}), bf16[128,2,288]{2,1,0:T(2,128)(2,1)S(1)}, u32[]{:S(2)}, u32[]{:S(2)}) async-start(bf16[128,2,288]{2,1,0:T(2,128)(2,1)} %reshape.81), calls=%async_computation.1 | async-start | bytes 393216 | tf_op jit(solution)/shard_map/all_to_all | solution.py:302
  41.7 11.1 %near.1 = (f32[16,3,128]{2,1,0:T(4,128)S(1)}, f32[48,3,128]{2,1,0:T(4,128)S(1)}) custom-call(s32[128]{0:T(128)S(1)} %reshape.59.idx_ref, s32[16]{0:T(128)S(1)} %copy-done.1, f32[48,8,128]{2,1,0:T(8,128)S(1)} %pad.4.win_ref), custom_call_target="tpu_custom_call" | custom-call | flops 100000000 | bytes 1000000 | tf_op jit(solution)/shard_map/near/pallas_call | solution.py:96
  52.8 3.8 %collective-permute-start.3 = (f32[16,3,128]{2,1,0:T(4,128)S(1)}, f32[16,3,128]{2,1,0:T(4,128)S(1)}, u32[]{:S(2)}, u32[]{:S(2)}) collective-permute-start(f32[16,3,128]{2,1,0:T(4,128)S(1)} %get-tuple-element.10), channel_id=1, source_target_pairs={{0,1},{1,2},{2,3},{3,4},{4,5},{5,6},{6,7},{7,8},{8,9},{9,10},{10,1... | collective-permute-start | bytes 73736 | tf_op jit(solution)/shard_map/ppermute | solution.py:34
  56.7 8.1 %collective-permute-start.2 = (f32[16,3,128]{2,1,0:T(4,128)S(1)}, f32[16,3,128]{2,1,0:T(4,128)S(1)}, u32[]{:S(2)}, u32[]{:S(2)}) collective-permute-start(f32[16,3,128]{2,1,0:T(4,128)S(1)} %get-tuple-element.9), channel_id=1, source_target_pairs={{1,0},{2,1},{3,2},{4,3},{5,4},{6,5},{7,6},{8,7},{9,8},{10,9},{11,1... | collective-permute-start | bytes 73736 | tf_op jit(solution)/shard_map/ppermute | solution.py:34
  64.8 0.6 slice.18.dens_ref
  65.4 0.7 reshape.61.slot_ref
  66.1 0.6 reshape.62.class_ref
  66.7 8.6 %copy.23.basis_hbm = bf16[16,144,9,128]{3,2,1,0:T(8,128)(2,1)} copy(bf16[16,144,9,128]{3,1,2,0:T(8,128)(2,1)} %param.24) | data formatting | bytes 10616832 | tf_op args[10]
  75.5 1.0 reduce
  76.5 1.0 reshape.64.mom_ref
  77.5 28.1 %far.1 = f32[16,3,128]{2,1,0:T(4,128)} custom-call(s32[512]{0:T(512)} %reshape.61.slot_ref, s32[512]{0:T(512)} %reshape.62.class_ref, s32[16]{0:T(128)} %cnt_ref.3, bf16[512,144]{1,0:T(8,128)(2,1)} %reshape.64.mom_ref, bf16[144,1152]{1,0:T(8,128)(2,1)} %constant.21.clone.sel_ref, bf16[1152,128]{1,0:T(8,128)(2,1)} %constant.22.clone.seg_ref, ...), custom_call_target="tpu_custom_call" | custom-call | flops 100000000 | bytes 20000000 | tf_op jit(solution)/shard_map/far/pallas_call | solution.py:250
  105.6 1.4 %add_bitcast_fusion = f32[3,2048]{1,0:T(4,128)} fusion(f32[16,3,128]{2,1,0:T(4,128)} %far.1, f32[16,3,128]{2,1,0:T(4,128)S(1)} %collective-permute-done.3, f32[16,3,128]{2,1,0:T(4,128)S(1)} %collective-permute-done.2, f32[16,3,128]{2,1,0:T(4,128)S(1)} %get-tuple-element.7, f32[48,3,128]{2,1,0:T(4,128)S(1)} %get-tuple-element.8), kind=kLoop, calls=%fused_computation.4 | loop fusion | flops 24576 | bytes 147456 | tf_op jit(solution)/shard_map/reshape | solution.py:314
  (32 shorter events, 0.7 us)
Async XLA Ops:
  0.0 21.8 %copy-start = (bf16[16,144,384]{2,1,0:T(8,128)(2,1)S(1)}, bf16[16,144,384]{2,1,0:T(8,128)(2,1)}, u32[]{:S(2)}) copy-start(bf16[16,144,384]{2,1,0:T(8,128)(2,1)} %param.22) | copy-start | bytes 5308420
  0.0 22.5 %copy-start.6 = (s32[16,8]{0,1:T(8,128)S(1)}, s32[16,8]{0,1:T(8,128)}, u32[]{:S(2)}) copy-start(s32[16,8]{0,1:T(8,128)} %param.16) | copy-start | bytes 1540
  0.9 40.7 %collective-permute-start.1 = (f32[6,2048]{1,0:T(8,128)S(1)}, f32[6,2048]{1,0:T(8,128)S(1)}, u32[]{:S(2)}, u32[]{:S(2)}) collective-permute-start(f32[6,2048]{1,0:T(8,128)S(1)} %get-tuple-element.11), channel_id=1, source_target_pairs={{1,0},{2,1},{3,2},{4,3},{5,4},{6,5},{7,6},{8,7},{9,8},{10,9},{11,1... | collective-permute-start | bytes 147464 | tf_op jit(solution)/shard_map/ppermute | solution.py:26
  8.4 33.2 %collective-permute-start = (f32[6,2048]{1,0:T(8,128)S(1)}, f32[6,2048]{1,0:T(8,128)S(1)}, u32[]{:S(2)}, u32[]{:S(2)}) collective-permute-start(f32[6,2048]{1,0:T(8,128)S(1)} %get-tuple-element.11), channel_id=1, source_target_pairs={{0,1},{1,2},{2,3},{3,4},{4,5},{5,6},{6,7},{7,8},{8,9},{9,10},{10,1... | collective-permute-start | bytes 147464 | tf_op jit(solution)/shard_map/ppermute | solution.py:25
  11.8 19.0 %all-to-all-start = ((s32[128,1,4]{2,1,0:T(1,128)}), s32[128,1,4]{2,1,0:T(1,128)S(1)}, u32[]{:S(2)}, u32[]{:S(2)}) async-start(s32[128,1,4]{2,1,0:T(1,128)} %bitcast.5), calls=%async_computation | async-start | bytes 131072 | tf_op jit(solution)/shard_map/all_to_all | solution.py:300
  30.9 10.8 %copy-start.2 = (f32[3,2048]{1,0:T(4,128)S(1)}, f32[3,2048]{1,0:T(4,128)}, u32[]{:S(2)}) copy-start(f32[3,2048]{1,0:T(4,128)} %param.15) | copy-start | bytes 73732
  30.9 10.8 %copy-start.3 = (f32[3,2048]{1,0:T(4,128)S(1)}, f32[3,2048]{1,0:T(4,128)}, u32[]{:S(2)}) copy-start(f32[3,2048]{1,0:T(4,128)} %param.14) | copy-start | bytes 73732
  32.9 8.9 %copy-start.1 = (s32[16]{0:T(128)S(1)}, s32[16]{0:T(128)}, u32[]{:S(2)}) copy-start(s32[16]{0:T(128)} %cnt_ref.2) | copy-start | bytes 196
  35.5 29.9 %copy-start.4 = (s32[16,32]{1,0:T(8,128)S(1)}, s32[16,32]{1,0:T(8,128)}, u32[]{:S(2)}) copy-start(s32[16,32]{1,0:T(8,128)} %param.18) | copy-start | bytes 6148
  35.5 30.5 %copy-start.5 = (s32[16,32]{1,0:T(8,128)S(1)}, s32[16,32]{1,0:T(8,128)}, u32[]{:S(2)}) copy-start(s32[16,32]{1,0:T(8,128)} %param.19) | copy-start | bytes 6148
  36.4 38.8 %all-to-all-start.1 = ((bf16[128,2,288]{2,1,0:T(2,128)(2,1)}), bf16[128,2,288]{2,1,0:T(2,128)(2,1)S(1)}, u32[]{:S(2)}, u32[]{:S(2)}) async-start(bf16[128,2,288]{2,1,0:T(2,128)(2,1)} %reshape.81), calls=%async_computation.1 | async-start | bytes 393216 | tf_op jit(solution)/shard_map/all_to_all | solution.py:302
  52.8 52.7 %collective-permute-start.3 = (f32[16,3,128]{2,1,0:T(4,128)S(1)}, f32[16,3,128]{2,1,0:T(4,128)S(1)}, u32[]{:S(2)}, u32[]{:S(2)}) collective-permute-start(f32[16,3,128]{2,1,0:T(4,128)S(1)} %get-tuple-element.10), channel_id=1, source_target_pairs={{0,1},{1,2},{2,3},{3,4},{4,5},{5,6},{6,7},{7,8},{8,9},{9,10},{10,1... | collective-permute-start | bytes 73736 | tf_op jit(solution)/shard_map/ppermute | solution.py:34
  56.7 48.9 %collective-permute-start.2 = (f32[16,3,128]{2,1,0:T(4,128)S(1)}, f32[16,3,128]{2,1,0:T(4,128)S(1)}, u32[]{:S(2)}, u32[]{:S(2)}) collective-permute-start(f32[16,3,128]{2,1,0:T(4,128)S(1)} %get-tuple-element.9), channel_id=1, source_target_pairs={{1,0},{2,1},{3,2},{4,3},{5,4},{6,5},{7,6},{8,7},{9,8},{10,9},{11,1... | collective-permute-start | bytes 73736 | tf_op jit(solution)/shard_map/ppermute | solution.py:34

commit v2 on v0

v2 whole, which is shorter than its diff:
```python
import functools
import math

import jax
import jax.numpy as jnp
import numpy as np
from jax import lax
from jax.experimental import pallas as pl
from jax.experimental.pallas import tpu as pltpu
from jax.sharding import PartitionSpec as P

KERNEL = 1.0 / (8.0 * math.pi)
BLOB = 0.25
PITCH = 9
SIDE = 4
F32 = jnp.float32
BF16 = jnp.bfloat16
MESH = pl.DeviceIdType.MESH
SMEM = pl.BlockSpec(memory_space=pltpu.SMEM)
VMEM = pl.BlockSpec(memory_space=pltpu.VMEM)
HBM = pl.BlockSpec(memory_space=pltpu.HBM)


def exchange_kernel(
    count, pos_ref, den_ref, up_hbm, wpos_ref, wden_ref, mom_ref, up, up_sem, own_sem, halo_send, halo_recv,
    send_sem, recv_sem, fwd_send, fwd_recv
):
    leaves, width = up.shape[0], up.shape[1]
    chips = SIDE * SIDE * SIDE
    plane = SIDE * SIDE
    me = lax.axis_index("patch")
    core = me % 2
    chip = me // 2
    y, z, x = chip // plane, (chip // SIDE) % SIDE, chip % SIDE
    partner = me + 1 - 2 * core
    other = (me + 2 * core - 1 + count) % count
    before = (me + count - 1) % count
    after = (me + 1) % count

    def peer(k):
        ty = (y + k // plane) % SIDE
        tz = (z + (k // SIDE) % SIDE) % SIDE
        tx = (x + k % SIDE) % SIDE
        return ((ty * SIDE + tz) * SIDE + tx) * 2 + core

    get_up = pltpu.make_async_copy(up_hbm, up, up_sem)
    get_up.start()
    barrier = pltpu.get_barrier_semaphore()

    def greet(k, _):
        pl.semaphore_signal(barrier, inc=1, device_id=(peer(k),), device_id_type=MESH)
        return 0

    pl.semaphore_signal(barrier, inc=1, device_id=(partner,), device_id_type=MESH)
    pl.semaphore_signal(barrier, inc=1, device_id=(other,), device_id_type=MESH)
    lax.fori_loop(1, chips, greet, 0)

    own = []
    for i, (src, dst) in enumerate(((pos_ref, wpos_ref), (den_ref, wden_ref))):
        dst[pl.ds(leaves, leaves)] = src[...]

    rounded = jnp.concatenate([den_ref[:, c, :] for c in range(3)], axis=1)
    row = lax.broadcasted_iota(jnp.int32, rounded.shape, 0)
    get_up.wait()
    total = jnp.zeros((leaves, width), F32)
    for leaf in range(leaves):
        only = jnp.where(row == leaf, rounded, 0.0).astype(BF16)
        total = total + lax.dot_general(
            only, up[leaf], (((1,), (1,)), ((), ())), preferred_element_type=F32
        )
    pad = jnp.zeros((leaves, mom_ref.shape[-1] - width), F32)
    mom_ref[core, y, z * SIDE + x] = jnp.concatenate([total, pad], axis=1).astype(BF16)

    pl.semaphore_wait(barrier, chips + 1)
    halos = []
    for i, (src, dst) in enumerate(((pos_ref, wpos_ref), (den_ref, wden_ref))):
        for j, (target, at) in enumerate(((before, 2 * leaves), (after, 0))):
            halos.append(
                pltpu.make_async_remote_copy(
                    src_ref=src,
                    dst_ref=dst.at[pl.ds(at, leaves)],
                    send_sem=halo_send.at[2 * i + j],
                    recv_sem=halo_recv.at[2 * i + j],
                    device_id=(target,),
                    device_id_type=MESH,
                )
            )
    for copy in halos:
        copy.start()
    mine = mom_ref.at[core, y, z * SIDE + x]

    def send(k, _):
        pltpu.make_async_remote_copy(
            src_ref=mine,
            dst_ref=mine,
            send_sem=send_sem,
            recv_sem=recv_sem.at[k // plane],
            device_id=(peer(k),),
            device_id_type=MESH,
        ).start()
        return 0

    lax.fori_loop(1, chips, send, 0)
    forwards = []
    for group in range(SIDE):
        from_y = (y + SIDE - group) % SIDE
        got = mom_ref.at[core, from_y]
        part = mom_ref.at[core, from_y, pl.ds(0, plane - 1)] if group == 0 else got
        pltpu.make_async_copy(part, part, recv_sem.at[group]).wait()
        forwards.append(
            pltpu.make_async_remote_copy(
                src_ref=got,
                dst_ref=got,
                send_sem=fwd_send.at[group],
                recv_sem=fwd_recv.at[group],
                device_id=(partner,),
                device_id_type=MESH,
            )
        )
        forwards[-1].start()
    for copy in halos + forwards:
        copy.wait()
    sent = mom_ref.at[core, pl.ds(0, SIDE - 1)]
    pltpu.make_async_copy(sent, sent, send_sem).wait()
    sent = mom_ref.at[core, 0, pl.ds(0, plane - 1)]
    pltpu.make_async_copy(sent, sent, send_sem).wait()


def exchange_call(count, pos, den, up):
    leaves, rows, lanes = pos.shape
    return pl.pallas_call(
        functools.partial(exchange_kernel, count),
        name="exchange",
        out_shape=(
            jax.ShapeDtypeStruct((3 * leaves, rows, lanes), F32),
            jax.ShapeDtypeStruct((3 * leaves, rows, lanes), F32),
            jax.ShapeDtypeStruct((2, SIDE, SIDE * SIDE, leaves, 256), BF16),
        ),
        in_specs=[VMEM, VMEM, HBM],
        out_specs=(VMEM, VMEM, VMEM),
        scratch_shapes=[
            pltpu.VMEM(up.shape, BF16),
            pltpu.SemaphoreType.DMA,
            pltpu.SemaphoreType.DMA((2,)),
            pltpu.SemaphoreType.DMA((4,)),
            pltpu.SemaphoreType.DMA((4,)),
            pltpu.SemaphoreType.DMA,
            pltpu.SemaphoreType.DMA((SIDE,)),
            pltpu.SemaphoreType.DMA((SIDE,)),
            pltpu.SemaphoreType.DMA((SIDE,)),
        ],
        compiler_params=pltpu.CompilerParams(
            collective_id=0, has_side_effects=True, vmem_limit_bytes=24 << 20
        ),
    )(pos, den, up)


def near_blocks(near_ref, cnt_ref, wpos_ref, wden_ref, tgt_ref, bef_ref, aft_ref, cols, racc, sacc):
    leaves = tgt_ref.shape[0]
    shift = (lax.axis_index("patch") - 1) * leaves
    tiles = 128 // 8
    sacc[...] = jnp.zeros_like(sacc)

    def spread(pair, _):
        for sub in range(2):
            leaf = pair * 2 + sub
            rows = jnp.concatenate(
                [wpos_ref[leaves + leaf], wden_ref[leaves + leaf], jnp.zeros((2, 128), F32)], axis=0
            )
            turned = jnp.transpose(rows, (1, 0))
            for k in range(6):
                cols[leaf, k] = jnp.broadcast_to(turned[:, k : k + 1], (128, 128))
        return 0

    lax.fori_loop(0, leaves // 2, spread, 0)

    def leaf_step(leaf, _):
        racc[leaf] = jnp.zeros_like(racc[leaf])

        def slot_step(slot, _):
            other = near_ref[slot, leaf] - shift
            xs3, fs3 = wpos_ref[other], wden_ref[other]
            xs = [jnp.broadcast_to(xs3[k : k + 1], (8, 128)) for k in range(3)]
            fs = [jnp.broadcast_to(fs3[k : k + 1], (8, 128)) for k in range(3)]
            down = [jnp.zeros((8, 128), F32) for _ in range(3)]
            for tile in range(tiles):
                part = pl.ds(8 * tile, 8)
                fa = [cols[leaf, 3 + k, part] for k in range(3)]
                sep = [cols[leaf, k, part] - xs[k] for k in range(3)]
                rho = (sep[0] * sep[0] + sep[1] * sep[1]) + (sep[2] * sep[2] + BLOB)
                inv = lax.rsqrt(rho)
                inv_two = inv * inv
                inv_three = inv_two * inv
                ab = fa[0] * fs[0] + fa[1] * fs[1] + fa[2] * fs[2]
                ar = fa[0] * sep[0] + fa[1] * sep[1] + fa[2] * sep[2]
                br = fs[0] * sep[0] + fs[1] * sep[1] + fs[2] * sep[2]
                on_b = ar * inv_three
                on_a = br * inv_three
                on_r = ab * inv_three + (on_b * br) * (inv_two * 3.0)
                for k in range(3):
                    term = fa[k] * on_a + fs[k] * on_b - on_r * sep[k]
                    racc[leaf, k, part] += term
                    down[k] = down[k] + term
            for k in range(3):
                sacc[other, k] -= down[k]
            return 0

        lax.fori_loop(0, cnt_ref[leaf], slot_step, 0)
        return 0

    lax.fori_loop(0, leaves, leaf_step, 0)

    def gather(pair, _):
        for sub in range(2):
            leaf = pair * 2 + sub
            for k in range(3):
                turned = jnp.transpose(racc[leaf, k], (1, 0))
                folded = turned[0:8]
                for tile in range(1, tiles):
                    folded = folded + turned[8 * tile : 8 * tile + 8]
                folded = folded + sacc[leaves + leaf, k]
                row = pl.ds(k, 1)
                tgt_ref[leaf, row] = jnp.sum(folded, axis=0, keepdims=True) * KERNEL
                bef_ref[leaf, row] = jnp.sum(sacc[leaf, k], axis=0, keepdims=True) * KERNEL
                aft_ref[leaf, row] = (
                    jnp.sum(sacc[2 * leaves + leaf, k], axis=0, keepdims=True) * KERNEL
                )
        return 0

    lax.fori_loop(0, leaves // 2, gather, 0)


def middle_kernel(
    near_ref, cnt_ref, slot_ref, class_ref, fcnt_ref, req_ref, wpos_ref, wden_ref, mom_ref, sel_ref, seg_ref, table_hbm,
    tgt_ref, bef_ref, aft_ref, exp_ref, cols, racc, sacc, table, wide, pattern, sums, place, base, sem
):
    leaves = tgt_ref.shape[0]
    classes = table_hbm.shape[0]
    chunks = table_hbm.shape[1] // 128
    get_table = pltpu.make_async_copy(table_hbm, table, sem)
    get_table.start()

    def lookup(leaf, _):
        for slot in range(32):
            v = slot_ref[leaf, slot]
            kind = class_ref[leaf, slot]
            who = v >> 2
            which = req_ref[v & 3, who]
            place[leaf * 32 + slot] = ((who & 1) * (SIDE * SIDE * SIDE) + (who >> 1)) * leaves + which
            base[leaf * 32 + slot] = (kind >> 3) * (chunks * PITCH) + (kind & 7)
        return 0

    lax.fori_loop(0, leaves, lookup, 0)
    near_blocks(near_ref, cnt_ref, wpos_ref, wden_ref, tgt_ref, bef_ref, aft_ref, cols, racc, sacc)

    def spread(step, _):
        rows = pl.ds(pl.multiple_of(step * 128, 128), 128)
        for v in range(9):
            part = sel_ref[:, 128 * v : 128 * v + 128]
            pattern[v, rows] = jnp.dot(mom_ref[rows], part, preferred_element_type=F32)
        return 0

    lax.fori_loop(0, mom_ref.shape[0] // 128, spread, 0)
    get_table.wait()

    def widen(block, _):
        rows = pl.ds(pl.multiple_of(block * 8, 8), 8)
        at = block * (chunks * PITCH)
        for chunk in range(chunks):
            wide[pl.ds(at + chunk * PITCH, 8)] = table[rows, 128 * chunk : 128 * chunk + 128].astype(F32)
        return 0

    full = classes // 8
    rest = classes - 8 * full
    lax.fori_loop(0, full, widen, 0)
    if rest:
        at = full * chunks * PITCH
        for chunk in range(chunks):
            wide[at + chunk * PITCH : at + chunk * PITCH + rest] = table[
                8 * full :, 128 * chunk : 128 * chunk + 128
            ].astype(F32)

    def leaf_step(leaf, _):
        def slot_step(slot, carry):
            at, start, acc = carry
            new = []
            for v in range(9):
                p = jnp.broadcast_to(pattern[v, pl.ds(at, 1), :], (8, 128))
                for g in range(3):
                    t = wide[pl.ds(start + (72 * g + v) * PITCH, 8, stride=9 * PITCH), :]
                    new.append(acc[3 * v + g] + p * t)
            index = jnp.minimum(leaf * 32 + slot + 1, leaves * 32 - 1)
            return place[index], base[index], tuple(new)

        zero = jnp.zeros((8, 128), F32)
        first = leaf * 32
        _, _, acc = lax.fori_loop(0, fcnt_ref[leaf], slot_step, (place[first], base[first], (zero,) * 27))
        for v in range(9):
            for g in range(3):
                rows = pl.ds(pl.multiple_of(leaf * 24 + 8 * g, 8), 8)
                sums[v, rows] = acc[3 * v + g]
        return 0

    lax.fori_loop(0, leaves, leaf_step, 0)
    result = jnp.zeros((leaves * 24, seg_ref.shape[1]), F32)
    for v in range(9):
        total = sums[v]
        high = total.astype(BF16)
        low = (total - high.astype(F32)).astype(BF16)
        part = seg_ref[128 * v : 128 * v + 128]
        result = result + jnp.dot(high, part, preferred_element_type=F32)
        result = result + jnp.dot(low, part, preferred_element_type=F32)
    group = lax.broadcasted_iota(jnp.int32, (24, seg_ref.shape[1]), 0)
    lane = lax.broadcasted_iota(jnp.int32, (24, seg_ref.shape[1]), 1)
    keep = group == (lane >> 3)
    rows = []
    for leaf in range(leaves):
        mine = jnp.where(keep, result[24 * leaf : 24 * leaf + 24], 0.0)
        rows.append(jnp.sum(mine, axis=0, keepdims=True))
    out = jnp.concatenate(rows, axis=0).astype(BF16)
    exp_ref[...] = out[:, : exp_ref.shape[1]]


def middle_consts(width):
    flat = np.arange(9 * 128)
    sel = (flat[None, :] % width == np.arange(256)[:, None]).astype(np.float32)
    seg = (flat[:, None] // width == np.arange(256)[None, :] % 8).astype(np.float32)
    return [jnp.asarray(m, BF16) for m in (sel, seg)]


def middle_call(near, cnt, slots, kinds, fcnt, requests, wpos, wden, mom, table, width):
    leaves = cnt.shape[0]
    classes = table.shape[0]
    chunks = table.shape[1] // 128
    blocks = -(-classes // 8)
    sel, seg = middle_consts(width)
    grad = jax.ShapeDtypeStruct((leaves, 3, 128), F32)
    return pl.pallas_call(
        middle_kernel,
        name="middle",
        out_shape=(grad, grad, grad, jax.ShapeDtypeStruct((leaves, width), BF16)),
        in_specs=[SMEM] * 6 + [VMEM] * 5 + [HBM],
        out_specs=(VMEM,) * 4,
        scratch_shapes=[
            pltpu.VMEM((leaves, 6, 128, 128), F32),
            pltpu.VMEM((leaves, 3, 128, 128), F32),
            pltpu.VMEM((3 * leaves, 3, 8, 128), F32),
            pltpu.VMEM(table.shape, BF16),
            pltpu.VMEM(((blocks * chunks + 54) * PITCH, 128), F32),
            pltpu.VMEM((9, mom.shape[0], 128), F32),
            pltpu.VMEM((9, leaves * 24, 128), F32),
            pltpu.SMEM((leaves * 32,), jnp.int32),
            pltpu.SMEM((leaves * 32,), jnp.int32),
            pltpu.SemaphoreType.DMA,
        ],
        compiler_params=pltpu.CompilerParams(vmem_limit_bytes=60 << 20),
        cost_estimate=pl.CostEstimate(flops=10**8, bytes_accessed=10**7, transcendentals=10**6),
    )(near, cnt, slots, kinds, fcnt, requests, wpos, wden, mom, sel, seg, table)


def final_kernel(
    count, exp_ref, den_ref, tgt_ref, bef_ref, aft_ref, basis_hbm, out_ref, basis, got, sem, send_sem, recv_sem
):
    leaves, parts = basis.shape[0], basis.shape[1]
    me = lax.axis_index("patch")
    before = (me + count - 1) % count
    after = (me + 1) % count
    half = leaves // 2
    gets = []
    for i in range(2):
        part = pl.ds(half * i, half)
        gets.append(pltpu.make_async_copy(basis_hbm.at[part], basis.at[part], sem.at[i]))
        gets[-1].start()
    barrier = pltpu.get_barrier_semaphore()
    for target in (before, after):
        pl.semaphore_signal(barrier, inc=1, device_id=(target,), device_id_type=MESH)
    pl.semaphore_wait(barrier, 2)
    copies = []
    for i, (src, target) in enumerate(((bef_ref, before), (aft_ref, after))):
        copies.append(
            pltpu.make_async_remote_copy(
                src_ref=src,
                dst_ref=got.at[i],
                send_sem=send_sem.at[i],
                recv_sem=recv_sem.at[i],
                device_id=(target,),
                device_id_type=MESH,
            )
        )
        copies[-1].start()
    expansion = exp_ref[...]
    row = lax.broadcasted_iota(jnp.int32, expansion.shape, 0)
    field = [jnp.zeros((leaves, 128), F32) for _ in range(parts)]
    for leaf in range(leaves):
        if leaf % half == 0:
            gets[leaf // half].wait()
        only = jnp.where(row == leaf, expansion, jnp.zeros_like(expansion))
        for q in range(parts):
            field[q] = field[q] + jnp.dot(only, basis[leaf, q], preferred_element_type=F32)
    far = []
    for k in range(3):
        part = den_ref[:, 0, :] * field[k]
        for c in range(1, 3):
            part = part + den_ref[:, c, :] * field[3 * c + k]
        far.append(part)
    for copy in copies:
        copy.wait()
    for k in range(3):
        out_ref[:, k, :] = far[k] + (tgt_ref[:, k, :] + (got[0, :, k, :] + got[1, :, k, :]))


def final_call(count, expansion, den, tgt, bef, aft, basis):
    leaves = den.shape[0]
    return pl.pallas_call(
        functools.partial(final_kernel, count),
        name="final",
        out_shape=jax.ShapeDtypeStruct(den.shape, F32),
        in_specs=[VMEM] * 5 + [HBM],
        out_specs=VMEM,
        scratch_shapes=[
            pltpu.VMEM(basis.shape, BF16),
            pltpu.VMEM((2,) + den.shape, F32),
            pltpu.SemaphoreType.DMA((2,)),
            pltpu.SemaphoreType.DMA((2,)),
            pltpu.SemaphoreType.DMA((2,)),
        ],
        compiler_params=pltpu.CompilerParams(
            collective_id=1, has_side_effects=True, vmem_limit_bytes=24 << 20
        ),
    )(expansion, den, tgt, bef, aft, basis)


def per_device(
    count,
    positions,
    densities,
    near_src,
    near_count,
    far_slot,
    far_class,
    far_count,
    requests,
    up_basis,
    transfer_table,
    down_basis,
):
    leaves = near_count.shape[0]
    width = up_basis.shape[1]

    def by_leaf(a):
        return a.reshape(3, leaves, -1).transpose(1, 0, 2)

    pos, den = by_leaf(positions), by_leaf(densities)
    wpos, wden, mom = exchange_call(count, pos, den, up_basis)
    tgt, bef, aft, expansion = middle_call(
        near_src.T,
        near_count,
        far_slot,
        far_class,
        far_count,
        requests[0].T,
        wpos,
        wden,
        mom.reshape(-1, mom.shape[-1]),
        transfer_table,
        width,
    )
    out = final_call(count, expansion, den, tgt, bef, aft, down_basis.transpose(0, 2, 1, 3))
    return out.transpose(1, 0, 2).reshape(3, -1)


def solution(mesh):
    placed = (
        P(None, "patch"),
        P(None, "patch"),
        P("patch", None),
        P("patch"),
        P("patch", None),
        P("patch", None),
        P("patch"),
        P("patch", None, None),
        P("patch", None, None),
        P(),
        P("patch", None, None, None),
    )
    return jax.shard_map(
        functools.partial(per_device, mesh.shape["patch"]),
        mesh=mesh,
        in_specs=placed,
        out_specs=P(None, "patch"),
        check_vma=False,
    )
```

time: 241 us -> 74.7 us (0.31)
  the two profiles are of different devices: /device:TPU:8 before, /device:TPU:0 now
where the time goes in v2:
time: 74.7 us; the launch traced here: 74.2 us
  Pallas kernels  62.8 us (84%)
  local copies, waits for them, and re-layouts  11.3 us (15%)
    pallas_call x1, Pallas kernels, middle_call(): pl.pallas_call(middle_kernel, name='middle', out_shape=(grad, grad, grad,...  25.4 us
    pallas_call x1, Pallas kernels, exchange_call(): pl.pallas_call(functools.partial(exchange_kernel, count), name='exchange'...  21.7 us
    pallas_call x1, Pallas kernels, final_call(): pl.pallas_call(functools.partial(final_kernel, count), name='final', out_...  15.7 us
    unnamed x25, local copies, waits for them, and re-layouts  11.3 us

profile of v2, /device:TPU:0, one launch (start us, length us, event | category | flops | bytes accessed | tf_op | source)
XLA Modules:
  0.0 74.2 jit_solution(11889711152786928556)
XLA Ops:
  0.0 0.0 copy-start.1
  0.0 1.5 %copy-done.1 = bf16[16,144,384]{2,1,0:T(8,128)(2,1)S(1)} copy-done((bf16[16,144,384]{2,1,0:T(8,128)(2,1)S(1)}, bf16[16,144,384]{2,1,0:T(8,128)(2,1)}, u32[]{:S(2)}) %copy-start.1) | copy-done | bytes 1769496
  1.5 0.0 copy-start.3
  1.5 0.8 %copy-done.3 = f32[3,2048]{1,0:T(4,128)S(1)} copy-done((f32[3,2048]{1,0:T(4,128)S(1)}, f32[3,2048]{1,0:T(4,128)}, u32[]{:S(2)}) %copy-start.3) | copy-done | bytes 24600
  2.2 0.0 copy-start.7
  2.2 0.8 %copy-done.7 = f32[3,2048]{1,0:T(4,128)S(1)} copy-done((f32[3,2048]{1,0:T(4,128)S(1)}, f32[3,2048]{1,0:T(4,128)}, u32[]{:S(2)}) %copy-start.7) | copy-done | bytes 24600
  3.0 21.7 %exchange.1 = (f32[48,3,128]{2,1,0:T(4,128)S(1)}, f32[48,3,128]{2,1,0:T(4,128)S(1)}, bf16[2,4,16,16,256]{4,3,2,1,0:T(8,128)(2,1)S(1)}) custom-call(f32[16,3,128]{2,1,0:T(4,128)S(1)} %bitcast.20, f32[16,3,128]{2,1,0:T(4,128)S(1)} %bitcast.17, bf16[16,144,384]{2,1,0:T(8,128)(2,1)S(1)} %copy-done.1), custom_call_target="tpu_custom_call" | custom-call | tf_op jit(solution)/shard_map/exchange/pallas_call | solution.py:131
  24.7 0.0 copy-start.2
  24.7 1.0 %copy-done.2 = bf16[2,4,16,16,256]{4,3,2,1,0:T(8,128)(2,1)} copy-done((bf16[2,4,16,16,256]{4,3,2,1,0:T(8,128)(2,1)}, bf16[2,4,16,16,256]{4,3,2,1,0:T(8,128)(2,1)S(1)}, u32[]{:S(2)}) %copy-start.2) | copy-done | bytes 1048600
  25.7 0.0 copy-start.5
  25.7 0.6 copy-done.5
  26.3 0.0 copy-start.6
  26.3 0.6 copy-done.6
  27.0 0.0 copy-start.4
  27.0 25.4 %middle.1 = (f32[16,3,128]{2,1,0:T(4,128)}, f32[16,3,128]{2,1,0:T(4,128)}, f32[16,3,128]{2,1,0:T(4,128)}, bf16[16,144]{1,0:T(8,128)(2,1)}) custom-call(s32[8,16]{1,0:T(8,128)} %bitcast.21, s32[16]{0:T(128)} %cnt_ref.1, s32[16,32]{1,0:T(8,128)} %slot_ref.1, s32[16,32]{1,0:T(8,128)} %class_ref.1, s32[16]{0:T(128)} %fcnt_ref.1, s32[4,128]{1,0:T(4,128)} %bitcast.22, ...), custom_call_target="tpu_custom_call" | custom-call | flops 100000000 | bytes 10000000 | tf_op jit(solution)/shard_map/middle/pallas_call | solution.py:338
  52.4 0.0 copy-done.4
  52.4 0.0 copy-start
  52.4 2.5 %copy-done = bf16[16,144,9,128]{3,1,2,0:T(8,128)(2,1)S(1)} copy-done((bf16[16,144,9,128]{3,1,2,0:T(8,128)(2,1)S(1)}, bf16[16,144,9,128]{3,1,2,0:T(8,128)(2,1)}, u32[]{:S(2)}) %copy-start) | copy-done | bytes 5308440
  54.9 0.8 %copy-done.8 = f32[16,3,128]{2,1,0:T(4,128)S(1)} copy-done((f32[16,3,128]{2,1,0:T(4,128)S(1)}, f32[16,3,128]{2,1,0:T(4,128)}, u32[]{:S(2)}) %copy-start.8) | copy-done | bytes 24600
  55.6 0.8 %copy-done.9 = f32[16,3,128]{2,1,0:T(4,128)S(1)} copy-done((f32[16,3,128]{2,1,0:T(4,128)S(1)}, f32[16,3,128]{2,1,0:T(4,128)}, u32[]{:S(2)}) %copy-start.9) | copy-done | bytes 24600
  56.4 0.8 %copy-done.10 = f32[16,3,128]{2,1,0:T(4,128)S(1)} copy-done((f32[16,3,128]{2,1,0:T(4,128)S(1)}, f32[16,3,128]{2,1,0:T(4,128)}, u32[]{:S(2)}) %copy-start.10) | copy-done | bytes 24600
  57.2 0.7 copy-done.11
  57.9 15.7 %final.1 = f32[16,3,128]{2,1,0:T(4,128)S(1)} custom-call(bf16[16,144]{1,0:T(8,128)(2,1)S(1)} %copy-done.11, f32[16,3,128]{2,1,0:T(4,128)S(1)} %bitcast.18, f32[16,3,128]{2,1,0:T(4,128)S(1)} %copy-done.8, f32[16,3,128]{2,1,0:T(4,128)S(1)} %copy-done.9, f32[16,3,128]{2,1,0:T(4,128)S(1)} %copy-done.10, bf16[16,9,144,128]{3,2,1,0:T(8,128)(2,1)S(1)} %bitcast.15), custom_call_target="tpu_custom_call" | custom-call | tf_op jit(solution)/shard_map/final/pallas_call | solution.py:414
  73.6 0.6 copy.15
  (4 shorter events, 0.0 us)
Async XLA Ops:
  0.0 1.5 %copy-start.1 = (bf16[16,144,384]{2,1,0:T(8,128)(2,1)S(1)}, bf16[16,144,384]{2,1,0:T(8,128)(2,1)}, u32[]{:S(2)}) copy-start(bf16[16,144,384]{2,1,0:T(8,128)(2,1)} %up_hbm.1) | copy-start | bytes 5308420
  1.5 0.8 %copy-start.3 = (f32[3,2048]{1,0:T(4,128)S(1)}, f32[3,2048]{1,0:T(4,128)}, u32[]{:S(2)}) copy-start(f32[3,2048]{1,0:T(4,128)} %param.14) | copy-start | bytes 73732
  2.2 0.8 %copy-start.7 = (f32[3,2048]{1,0:T(4,128)S(1)}, f32[3,2048]{1,0:T(4,128)}, u32[]{:S(2)}) copy-start(f32[3,2048]{1,0:T(4,128)} %param.13) | copy-start | bytes 73732
  24.7 1.0 %copy-start.2 = (bf16[2,4,16,16,256]{4,3,2,1,0:T(8,128)(2,1)}, bf16[2,4,16,16,256]{4,3,2,1,0:T(8,128)(2,1)S(1)}, u32[]{:S(2)}) copy-start(bf16[2,4,16,16,256]{4,3,2,1,0:T(8,128)(2,1)S(1)} %get-tuple-element.14) | copy-start | bytes 3145732
  25.7 0.6 copy-start.5
  26.3 0.6 copy-start.6
  27.0 25.4 %copy-start.4 = (f32[3,2048]{1,0:T(4,128)S(1)}, f32[3,2048]{1,0:T(4,128)}, u32[]{:S(2)}) copy-start(f32[3,2048]{1,0:T(4,128)} %param.14) | copy-start | bytes 73732
  52.4 2.5 %copy-start = (bf16[16,144,9,128]{3,1,2,0:T(8,128)(2,1)S(1)}, bf16[16,144,9,128]{3,1,2,0:T(8,128)(2,1)}, u32[]{:S(2)}) copy-start(bf16[16,144,9,128]{3,1,2,0:T(8,128)(2,1)} %param.23) | copy-start | bytes 15925252
  54.9 0.8 %copy-start.8 = (f32[16,3,128]{2,1,0:T(4,128)S(1)}, f32[16,3,128]{2,1,0:T(4,128)}, u32[]{:S(2)}) copy-start(f32[16,3,128]{2,1,0:T(4,128)} %get-tuple-element.16.tgt_ref) | copy-start | bytes 73732
  55.6 0.8 %copy-start.9 = (f32[16,3,128]{2,1,0:T(4,128)S(1)}, f32[16,3,128]{2,1,0:T(4,128)}, u32[]{:S(2)}) copy-start(f32[16,3,128]{2,1,0:T(4,128)} %get-tuple-element.17.bef_ref) | copy-start | bytes 73732
  56.4 0.8 %copy-start.10 = (f32[16,3,128]{2,1,0:T(4,128)S(1)}, f32[16,3,128]{2,1,0:T(4,128)}, u32[]{:S(2)}) copy-start(f32[16,3,128]{2,1,0:T(4,128)} %get-tuple-element.18.aft_ref) | copy-start | bytes 73732
  57.2 0.7 copy-start.11

commit v3 on v2

v3 whole, which is shorter than its diff:
```python
import functools
import math

import jax
import jax.numpy as jnp
import numpy as np
from jax import lax
from jax.experimental import pallas as pl
from jax.experimental.pallas import tpu as pltpu
from jax.sharding import PartitionSpec as P

KERNEL = 1.0 / (8.0 * math.pi)
BLOB = 0.25
PITCH = 9
SIDE = 4
F32 = jnp.float32
BF16 = jnp.bfloat16
MESH = pl.DeviceIdType.MESH
SMEM = pl.BlockSpec(memory_space=pltpu.SMEM)
VMEM = pl.BlockSpec(memory_space=pltpu.VMEM)
HBM = pl.BlockSpec(memory_space=pltpu.HBM)
MIB = 1 << 20
LIMIT = 8 * MIB


def in_hbm(*arrays):
    return [pltpu.with_memory_space_constraint(a, pltpu.HBM) for a in arrays]

EARLY = 4


def pair_block(leaf, source_x, source_f, cols, racc):
    xs = [jnp.broadcast_to(source_x[k : k + 1], (8, 128)) for k in range(3)]
    fs = [jnp.broadcast_to(source_f[k : k + 1], (8, 128)) for k in range(3)]
    down = [jnp.zeros((8, 128), F32) for _ in range(3)]
    for tile in range(16):
        part = pl.ds(8 * tile, 8)
        fa = [cols[leaf, 3 + k, part] for k in range(3)]
        sep = [cols[leaf, k, part] - xs[k] for k in range(3)]
        rho = (sep[0] * sep[0] + sep[1] * sep[1]) + (sep[2] * sep[2] + BLOB)
        inv = lax.rsqrt(rho)
        inv_two = inv * inv
        inv_three = inv_two * inv
        ab = fa[0] * fs[0] + fa[1] * fs[1] + fa[2] * fs[2]
        ar = fa[0] * sep[0] + fa[1] * sep[1] + fa[2] * sep[2]
        br = fs[0] * sep[0] + fs[1] * sep[1] + fs[2] * sep[2]
        on_b = ar * inv_three
        on_a = br * inv_three
        on_r = ab * inv_three + (on_b * br) * (inv_two * 3.0)
        for k in range(3):
            term = fa[k] * on_a + fs[k] * on_b - on_r * sep[k]
            racc[leaf, k, part] += term
            down[k] = down[k] + term
    return down


def exchange_kernel(
    count, near_ref, cnt_ref, pos_ref, den_ref, up_hbm, wpos_ref, wden_ref, mom_ref, cols, racc, early_ref, up, own, theirs,
    up_sem, pair_send, pair_recv, halo_send, halo_recv, send_sem, recv_sem
):
    leaves, width = up.shape[0], up.shape[1]
    plane = SIDE * SIDE
    chips = plane * SIDE
    me = lax.axis_index("patch")
    core = me % 2
    chip = me // 2
    y, z, x = chip // plane, (chip // SIDE) % SIDE, chip % SIDE
    partner = me + 1 - 2 * core
    other_side = (me + 2 * core - 1 + count) % count
    before = (me + count - 1) % count
    after = (me + 1) % count
    at_y = [((y + k) % SIDE) * (2 * plane) + core for k in range(SIDE)]
    at_z = [((z + k) % SIDE) * (2 * SIDE) for k in range(SIDE)]
    at_x = [((x + k) % SIDE) * 2 for k in range(SIDE)]
    steps = [(a, b, c) for a in range(SIDE) for b in range(SIDE) for c in range(SIDE)][1:]
    steps.sort(key=lambda s: -sum(min(v, SIDE - v) for v in s))
    peers = [at_y[a] + at_z[b] + at_x[c] for a, b, c in steps]

    get_up = pltpu.make_async_copy(up_hbm, up, up_sem)
    get_up.start()
    barrier = pltpu.get_barrier_semaphore()
    for target in [partner] + peers + [other_side]:
        pl.semaphore_signal(barrier, inc=1, device_id=(target,), device_id_type=MESH)

    wpos_ref[pl.ds(leaves, leaves)] = pos_ref[...]
    wden_ref[pl.ds(leaves, leaves)] = den_ref[...]
    rounded = jnp.concatenate([den_ref[:, c, :] for c in range(3)], axis=1)
    row = lax.broadcasted_iota(jnp.int32, rounded.shape, 0)

    def spread(pair, _):
        for sub in range(2):
            leaf = pair * 2 + sub
            rows = jnp.concatenate([pos_ref[leaf], den_ref[leaf], jnp.zeros((2, 128), F32)], axis=0)
            turned = jnp.transpose(rows, (1, 0))
            for k in range(6):
                cols[leaf, k] = jnp.broadcast_to(turned[:, k : k + 1], (128, 128))
        return 0

    get_up.wait()
    total = jnp.zeros((leaves, width), F32)
    for leaf in range(leaves):
        only = jnp.where(row == leaf, rounded, 0.0).astype(BF16)
        total = total + lax.dot_general(
            only, up[leaf], (((1,), (1,)), ((), ())), preferred_element_type=F32
        )
    main = total[:, :128]
    tail = jnp.concatenate([total[:, 128:]] * (128 // (width - 128)), axis=1)
    lane = lax.broadcasted_iota(jnp.int32, tail.shape, 1)
    leaf_of = lax.broadcasted_iota(jnp.int32, tail.shape, 0)
    per_row = 128 // (width - 128)
    tail = jnp.where(lane // (width - 128) == leaf_of % per_row, tail, 0.0)
    ends = [
        jnp.sum(tail[i * per_row : (i + 1) * per_row], axis=0, keepdims=True)
        for i in range(leaves // per_row)
    ]
    fill = jnp.zeros((8 - len(ends), 128), F32)
    own[...] = jnp.concatenate([main] + ends + [fill], axis=0).astype(BF16)
    lax.fori_loop(0, leaves // 2, spread, 0)
    racc[...] = jnp.zeros_like(racc)

    pl.semaphore_wait(barrier, chips + 1)
    to_partner = pltpu.make_async_remote_copy(
        src_ref=own,
        dst_ref=theirs,
        send_sem=pair_send,
        recv_sem=pair_recv,
        device_id=(partner,),
        device_id_type=MESH,
    )
    to_partner.start()
    halos = []
    for i, (src, dst) in enumerate(((pos_ref, wpos_ref), (den_ref, wden_ref))):
        for j, (target, at) in enumerate(((before, 2 * leaves), (after, 0))):
            halos.append(
                pltpu.make_async_remote_copy(
                    src_ref=src,
                    dst_ref=dst.at[pl.ds(at, leaves)],
                    send_sem=halo_send.at[2 * i + j],
                    recv_sem=halo_recv.at[2 * i + j],
                    device_id=(target,),
                    device_id_type=MESH,
                )
            )
    for copy in halos:
        copy.start()
    to_partner.wait_recv()
    mine, his = own[...].astype(F32), theirs[...].astype(F32)
    first = jnp.where(core == 0, mine, his)
    second = jnp.where(core == 0, his, mine)
    main_rows = leaves
    mom_ref[chip] = jnp.concatenate(
        [
            first[:main_rows],
            second[:main_rows],
            first[main_rows : main_rows + 2],
            second[main_rows : main_rows + 2],
            jnp.zeros((4, 128), F32),
        ],
        axis=0,
    ).astype(BF16)
    block = mom_ref.at[chip]
    for target in peers:
        pltpu.make_async_remote_copy(
            src_ref=block,
            dst_ref=block,
            send_sem=send_sem,
            recv_sem=recv_sem,
            device_id=(target,),
            device_id_type=MESH,
        ).start()
    for copy in halos:
        copy.wait()

    shift = (me - 1) * leaves

    def early(leaf, _):
        for slot in range(EARLY):
            source = jnp.clip(near_ref[slot, leaf] - shift, 0, 3 * leaves - 1)
            live = jnp.where(slot < cnt_ref[leaf], 1.0, 0.0)
            down = pair_block(leaf, wpos_ref[source], wden_ref[source] * live, cols, racc)
            early_ref[leaf, slot] = jnp.concatenate(
                [jnp.sum(d, axis=0, keepdims=True) for d in down], axis=0
            )
        return 0

    lax.fori_loop(0, leaves, early, 0)
    to_partner.wait_send()
    moved = mom_ref.at[pl.ds(0, chips - 1)]
    pltpu.make_async_copy(moved, moved, send_sem).wait()
    pltpu.make_async_copy(moved, moved, recv_sem).wait()


def exchange_call(count, near, cnt, pos, den, up):
    leaves, rows, lanes = pos.shape
    window = jax.ShapeDtypeStruct((3 * leaves, rows, lanes), F32)
    return pl.pallas_call(
        functools.partial(exchange_kernel, count),
        name="exchange",
        out_shape=(
            window,
            window,
            jax.ShapeDtypeStruct((count // 2, 40, 128), BF16),
            jax.ShapeDtypeStruct((leaves, 6, 128, 128), F32),
            jax.ShapeDtypeStruct((leaves, 3, 128, 128), F32),
            jax.ShapeDtypeStruct((leaves, EARLY, 3, 128), F32),
        ),
        in_specs=[SMEM, SMEM, VMEM, VMEM, HBM],
        out_specs=(VMEM,) * 6,
        scratch_shapes=[
            pltpu.VMEM(up.shape, BF16),
            pltpu.VMEM((24, 128), BF16),
            pltpu.VMEM((24, 128), BF16),
            pltpu.SemaphoreType.DMA,
            pltpu.SemaphoreType.DMA,
            pltpu.SemaphoreType.DMA,
            pltpu.SemaphoreType.DMA((4,)),
            pltpu.SemaphoreType.DMA((4,)),
            pltpu.SemaphoreType.DMA,
            pltpu.SemaphoreType.DMA,
        ],
        compiler_params=pltpu.CompilerParams(
            collective_id=0, has_side_effects=True, vmem_limit_bytes=LIMIT
        ),
    )(*in_hbm(near, cnt, pos, den, up))


def near_kernel(near_ref, cnt_ref, wpos_ref, wden_ref, cols, before_acc, early_ref, tgt_ref, bef_ref, aft_ref, racc, sacc):
    leaves = tgt_ref.shape[0]
    shift = (lax.axis_index("patch") - 1) * leaves
    sacc[...] = jnp.zeros_like(sacc)

    def leaf_step(leaf, _):
        racc[leaf] = jnp.zeros_like(racc[leaf])
        for slot in range(EARLY):
            other = near_ref[slot, leaf] - shift
            sacc[other, :, 0, :] += early_ref[leaf, slot]

        def slot_step(slot, _):
            other = near_ref[slot, leaf] - shift
            down = pair_block(leaf, wpos_ref[other], wden_ref[other], cols, racc)
            for k in range(3):
                sacc[other, k] += down[k]
            return 0

        lax.fori_loop(EARLY, cnt_ref[leaf], slot_step, 0)
        return 0

    lax.fori_loop(0, leaves, leaf_step, 0)

    def gather(pair, _):
        for sub in range(2):
            leaf = pair * 2 + sub
            for k in range(3):
                turned = jnp.transpose(racc[leaf, k] + before_acc[leaf, k], (1, 0))
                folded = turned[0:8]
                for tile in range(1, 16):
                    folded = folded + turned[8 * tile : 8 * tile + 8]
                folded = folded - sacc[leaves + leaf, k]
                row = pl.ds(k, 1)
                tgt_ref[leaf, row] = jnp.sum(folded, axis=0, keepdims=True) * KERNEL
                bef_ref[leaf, row] = jnp.sum(sacc[leaf, k], axis=0, keepdims=True) * -KERNEL
                aft_ref[leaf, row] = (
                    jnp.sum(sacc[2 * leaves + leaf, k], axis=0, keepdims=True) * -KERNEL
                )
        return 0

    lax.fori_loop(0, leaves // 2, gather, 0)


def near_call(near, cnt, wpos, wden, cols, racc, early):
    leaves = cnt.shape[0]
    grad = jax.ShapeDtypeStruct((leaves, 3, 128), F32)
    return pl.pallas_call(
        near_kernel,
        name="near",
        out_shape=(grad, grad, grad),
        in_specs=[SMEM] * 2 + [VMEM] * 5,
        out_specs=(VMEM,) * 3,
        scratch_shapes=[
            pltpu.VMEM((leaves, 3, 128, 128), F32),
            pltpu.VMEM((3 * leaves, 3, 8, 128), F32),
        ],
        compiler_params=pltpu.CompilerParams(vmem_limit_bytes=LIMIT),
        cost_estimate=pl.CostEstimate(flops=10**8, bytes_accessed=10**7, transcendentals=10**6),
    )(*in_hbm(near, cnt), wpos, wden, cols, racc, early)


def back_kernel(count, bef_ref, aft_ref, mom_ref, sel_ref, table, got, wide, pattern, send_sem, recv_sem):
    classes = table.shape[0]
    chunks = table.shape[1] // 128
    me = lax.axis_index("patch")
    before = (me + count - 1) % count
    after = (me + 1) % count
    barrier = pltpu.get_barrier_semaphore()
    for target in (before, after):
        pl.semaphore_signal(barrier, inc=1, device_id=(target,), device_id_type=MESH)
    pl.semaphore_wait(barrier, 2)
    copies = []
    for i, (src, target) in enumerate(((bef_ref, before), (aft_ref, after))):
        copies.append(
            pltpu.make_async_remote_copy(
                src_ref=src,
                dst_ref=got.at[i],
                send_sem=send_sem.at[i],
                recv_sem=recv_sem.at[i],
                device_id=(target,),
                device_id_type=MESH,
            )
        )
        copies[-1].start()
    lane = lax.broadcasted_iota(jnp.int32, (8, 128), 1)
    mine = lane // 16 == lax.broadcasted_iota(jnp.int32, (8, 128), 0)

    def spread(step, _):
        lefts, rights = [], []
        for sub in range(8):
            block = mom_ref[step * 8 + sub]
            lefts.append(block[:32])
            ends = block[32:40].astype(F32)
            for i in range(4):
                rights.append(jnp.where(mine, jnp.broadcast_to(ends[i : i + 1], (8, 128)), 0.0))
        lhs = jnp.concatenate(
            [jnp.concatenate(lefts, axis=0), jnp.concatenate(rights, axis=0).astype(BF16)], axis=1
        )
        rows = pl.ds(pl.multiple_of(step * 256, 256), 256)
        for v in range(0, 9, 2):
            some = min(2, 9 - v)
            out = jnp.dot(lhs, sel_ref[:, 128 * v : 128 * (v + some)], preferred_element_type=F32)
            for i in range(some):
                pattern[v + i, rows] = out[:, 128 * i : 128 * i + 128]
        return 0

    lax.fori_loop(0, mom_ref.shape[0] // 8, spread, 0)

    def widen(block, _):
        rows = pl.ds(pl.multiple_of(block * 8, 8), 8)
        at = block * (chunks * PITCH)
        for chunk in range(chunks):
            wide[pl.ds(at + chunk * PITCH, 8)] = table[rows, 128 * chunk : 128 * chunk + 128].astype(F32)
        return 0

    full = classes // 8
    rest = classes - 8 * full
    lax.fori_loop(0, full, widen, 0)
    if rest:
        at = full * chunks * PITCH
        for chunk in range(chunks):
            wide[at + chunk * PITCH : at + chunk * PITCH + rest] = table[
                8 * full :, 128 * chunk : 128 * chunk + 128
            ].astype(F32)
    for copy in copies:
        copy.wait()


def back_call(count, bef, aft, mom, table, width):
    leaves = bef.shape[0]
    chunks = table.shape[1] // 128
    blocks = -(-table.shape[0] // 8)
    sel, _ = constants(width)
    return pl.pallas_call(
        functools.partial(back_kernel, count),
        name="back",
        out_shape=(
            jax.ShapeDtypeStruct((2,) + bef.shape, F32),
            jax.ShapeDtypeStruct(((blocks * chunks + 54) * PITCH, 128), F32),
            jax.ShapeDtypeStruct((9, count * leaves, 128), F32),
        ),
        in_specs=[VMEM] * 5,
        out_specs=(VMEM,) * 3,
        scratch_shapes=[
            pltpu.SemaphoreType.DMA((2,)),
            pltpu.SemaphoreType.DMA((2,)),
        ],
        compiler_params=pltpu.CompilerParams(
            collective_id=1, has_side_effects=True, vmem_limit_bytes=LIMIT
        ),
    )(bef, aft, mom, sel, table)


def far_kernel(
    slot_ref, class_ref, fcnt_ref, req_ref, wide, pattern, seg_ref, basis, den_ref, tgt_ref, got, out_ref, sums
):
    leaves, parts = basis.shape[0], basis.shape[1]
    width = basis.shape[2]
    block_rows = width * width // 128 * PITCH

    def leaf_step(leaf, _):
        def fetch(slot):
            v = slot_ref[leaf, slot]
            kind = class_ref[leaf, slot]
            who = v >> 2
            return who * leaves + req_ref[v & 3, who], (kind >> 3) * block_rows + (kind & 7)

        def slot_step(slot, carry):
            at, start, acc = carry
            following = fetch(jnp.minimum(slot + 1, 31))
            new = []
            for v in range(9):
                p = jnp.broadcast_to(pattern[v, pl.ds(at, 1), :], (8, 128))
                for g in range(3):
                    t = wide[pl.ds(start + (72 * g + v) * PITCH, 8, stride=9 * PITCH), :]
                    new.append(acc[3 * v + g] + p * t)
            return following[0], following[1], tuple(new)

        zero = jnp.zeros((8, 128), F32)
        at, start = fetch(0)
        _, _, acc = lax.fori_loop(0, fcnt_ref[leaf], slot_step, (at, start, (zero,) * 27))
        for v in range(9):
            for g in range(3):
                rows = pl.ds(pl.multiple_of(leaf * 24 + 8 * g, 8), 8)
                sums[v, rows] = acc[3 * v + g]
        return 0

    lax.fori_loop(0, leaves, leaf_step, 0)
    result = jnp.zeros((leaves * 24, seg_ref.shape[1]), F32)
    for v in range(9):
        total = sums[v]
        high = total.astype(BF16)
        low = (total - high.astype(F32)).astype(BF16)
        part = seg_ref[128 * v : 128 * v + 128]
        result = result + jnp.dot(high, part, preferred_element_type=F32)
        result = result + jnp.dot(low, part, preferred_element_type=F32)
    group = lax.broadcasted_iota(jnp.int32, (24, seg_ref.shape[1]), 0)
    lane = lax.broadcasted_iota(jnp.int32, (24, seg_ref.shape[1]), 1)
    keep = group == (lane >> 3)
    rows = []
    for leaf in range(leaves):
        mine = jnp.where(keep, result[24 * leaf : 24 * leaf + 24], 0.0)
        rows.append(jnp.sum(mine, axis=0, keepdims=True))
    expansion = jnp.concatenate(rows, axis=0)[:, :width].astype(BF16)
    row = lax.broadcasted_iota(jnp.int32, expansion.shape, 0)
    field = [jnp.zeros((leaves, 128), F32) for _ in range(parts)]
    for leaf in range(leaves):
        only = jnp.where(row == leaf, expansion, jnp.zeros_like(expansion))
        for q in range(parts):
            field[q] = field[q] + jnp.dot(only, basis[leaf, q], preferred_element_type=F32)
    for k in range(3):
        far = den_ref[:, 0, :] * field[k]
        for c in range(1, 3):
            far = far + den_ref[:, c, :] * field[3 * c + k]
        out_ref[:, k, :] = far + (tgt_ref[:, k, :] + (got[0, :, k, :] + got[1, :, k, :]))


def constants(width):
    flat = np.arange(9 * 128)
    sel = np.zeros((256, 9 * 128), np.float32)
    place = flat % width
    sel[:128] = place[None, :] == np.arange(128)[:, None]
    sel[128:] = (place[None, :] >= 128) & ((place[None, :] - 128) == np.arange(128)[:, None] % (width - 128))
    seg = (flat[:, None] // width == np.arange(256)[None, :] % 8).astype(np.float32)
    return [jnp.asarray(m, BF16) for m in (sel, seg)]


def far_call(slots, kinds, fcnt, requests, wide, pattern, basis, den, tgt, got):
    leaves = den.shape[0]
    _, seg = constants(basis.shape[2])
    return pl.pallas_call(
        far_kernel,
        name="far",
        out_shape=jax.ShapeDtypeStruct(den.shape, F32),
        in_specs=[SMEM] * 4 + [VMEM] * 7,
        out_specs=VMEM,
        scratch_shapes=[pltpu.VMEM((9, leaves * 24, 128), F32)],
        compiler_params=pltpu.CompilerParams(vmem_limit_bytes=LIMIT),
        cost_estimate=pl.CostEstimate(flops=10**8, bytes_accessed=10**7, transcendentals=0),
    )(slots, kinds, fcnt, requests, wide, pattern, seg, basis, den, tgt, got)


def per_device(
    count,
    positions,
    densities,
    near_src,
    near_count,
    far_slot,
    far_class,
    far_count,
    requests,
    up_basis,
    transfer_table,
    down_basis,
):
    leaves = near_count.shape[0]
    width = up_basis.shape[1]

    def by_leaf(a):
        return a.reshape(3, leaves, -1).transpose(1, 0, 2)

    pos, den = by_leaf(positions), by_leaf(densities)
    near = near_src.T
    wpos, wden, mom, cols, racc, early = exchange_call(count, near, near_count, pos, den, up_basis)
    tgt, bef, aft = near_call(near, near_count, wpos, wden, cols, racc, early)
    got, wide, pattern = back_call(count, bef, aft, mom, transfer_table, width)
    out = far_call(
        far_slot,
        far_class,
        far_count,
        requests[0].T,
        wide,
        pattern,
        down_basis.transpose(0, 2, 1, 3),
        den,
        tgt,
        got,
    )
    return out.transpose(1, 0, 2).reshape(3, -1)


def solution(mesh):
    placed = (
        P(None, "patch"),
        P(None, "patch"),
        P("patch", None),
        P("patch"),
        P("patch", None),
        P("patch", None),
        P("patch"),
        P("patch", None, None),
        P("patch", None, None),
        P(),
        P("patch", None, None, None),
    )
    return jax.shard_map(
        functools.partial(per_device, mesh.shape["patch"]),
        mesh=mesh,
        in_specs=placed,
        out_specs=P(None, "patch"),
        check_vma=False,
    )
```

time: 74.7 us -> 48.4 us (0.65)
  Pallas kernels: 62.8 us -> 47.4 us
  local copies, waits for them, and re-layouts: 11.3 us -> 0.06 us
    pallas_call x2 -> x3, Pallas kernels: 41.1 us -> 22.2 us  [the longest x1 9.69 us: far_call(): pl.pallas_call(far_kernel, name='far', out_shape=jax.ShapeDtypeStruct(den...]
    unnamed x25 -> x20, local copies, waits for them, and re-layouts: 11.3 us -> 0.06 us
    pallas_call x1, Pallas kernels: 21.7 us -> 25.2 us  [exchange_call(): pl.pallas_call(functools.partial(exchange_kernel, count), name='exchange'...]
where the time goes in v3:
time: 48.4 us; the launch traced here: 47.6 us
  Pallas kernels  47.4 us (98%)
    pallas_call x1, Pallas kernels, exchange_call(): pl.pallas_call(functools.partial(exchange_kernel, count), name='exchange'...  25.2 us
    pallas_call x1, Pallas kernels, far_call(): pl.pallas_call(far_kernel, name='far', out_shape=jax.ShapeDtypeStruct(den...  9.69 us
    pallas_call x1, Pallas kernels, back_call(): pl.pallas_call(functools.partial(back_kernel, count), name='back', out_sh...  9.02 us
    pallas_call x1, Pallas kernels, near_call(): pl.pallas_call(near_kernel, name='near', out_shape=(grad, grad, grad), in...  3.46 us

profile of v3, /device:TPU:0, one launch (start us, length us, event | category | flops | bytes accessed | tf_op | source)
XLA Modules:
  0.0 47.6 jit_solution(12344418848050827922)
XLA Ops:
  0.0 0.0 copy-start.1
  0.0 0.0 copy-start
  0.0 25.2 %exchange.1 = (f32[48,3,128]{2,1,0:T(4,128)S(1)}, f32[48,3,128]{2,1,0:T(4,128)S(1)}, bf16[64,40,128]{2,1,0:T(8,128)(2,1)S(1)}, f32[16,6,128,128]{3,2,1,0:T(8,128...) custom-call(s32[8,16]{1,0:T(8,128)} %bitcast.21, s32[16]{0:T(128)} %cnt_ref.3, ...), custom_call_target="tpu_custom_call" | custom-call | tf_op jit(solution)/shard_map/exchange/pallas_call | solution.py:196
  25.2 0.0 slice-start
  25.2 0.0 slice-start.1
  25.2 3.5 %near.1 = (f32[16,3,128]{2,1,0:T(4,128)S(1)}, f32[16,3,128]{2,1,0:T(4,128)S(1)}, f32[16,3,128]{2,1,0:T(4,128)S(1)}) custom-call(s32[8,16]{1,0:T(8,128)} %bitcast.22, s32[16]{0:T(128)} %cnt_ref.3, f32[48,3,128]{2,1,0:T(4,128)S(1)} %get-tuple-element.17.wpos_ref, f32[48,3,128]{2,1,0:T(4,128)S(1)} %get-tuple-element.18.wden_ref, ...), custom_call_target="tpu_custom_call" | custom-call | flops 100000000 | bytes 10000000 | tf_op jit(solution)/shard_map/near/pallas_call | solution.py:273
  28.7 0.0 copy-start.2
  28.7 0.0 copy-start.3
  28.7 0.0 copy-start.4
  28.7 0.0 copy-start.5
  28.7 0.0 copy-start.6
  28.8 0.0 copy-start.7
  28.8 0.0 copy-done.1
  28.8 0.0 copy-done
  28.8 9.0 %back.1 = (f32[2,16,3,128]{3,2,1,0:T(4,128)S(1)}, f32[35478,128]{1,0:T(8,128)S(1)}, f32[9,2048,128]{2,1,0:T(8,128)S(1)}) custom-call(f32[16,3,128]{2,1,0:T(4,128)S(1)} %get-tuple-element.22.bef_ref, f32[16,3,128]{2,1,0:T(4,128)S(1)} %get-tuple-element.23.aft_ref, bf16[64,40,128]{2,1,0:T(8,128)(2,1)S(1)} %get-tuple-element.24.mom_ref, ...), custom_call_target="tpu_custom_call" | custom-call | tf_op jit(solution)/shard_map/back/pallas_call | solution.py:360
  37.8 0.0 slice-done
  37.8 0.0 slice-done.1
  37.8 0.0 copy-done.2
  37.8 0.0 copy-done.3
  37.9 0.0 copy-done.4
  37.9 0.0 copy-done.5
  37.9 0.0 copy-done.6
  37.9 0.0 copy-done.7
  37.9 9.7 %far.1 = f32[16,3,128]{2,1,0:T(4,128)} custom-call(s32[16,32]{1,0:T(8,128)S(1)} %copy-done.4, s32[16,32]{1,0:T(8,128)S(1)} %copy-done.5, s32[16]{0:T(128)S(1)} %copy-done.7, s32[4,128]{1,0:T(4,128)S(1)} %bitcast.19, f32[35478,128]{1,0:T(8,128)S(1)} %get-tuple-element.25.wide, f32[9,2048,128]{2,1,0:T(8,128)S(1)} %get-tuple-element.26.pattern, ...), custom_call_target="tpu_custom_call" | custom-call | flops 100000000 | bytes 10000000 | tf_op jit(solution)/shard_map/far/pallas_call | solution.py:457
  (1 shorter events, 0.0 us)
Async XLA Ops:
  0.0 28.8 %copy-start.1 = (bf16[256,1152]{1,0:T(8,128)(2,1)S(1)}, bf16[256,1152]{1,0:T(8,128)(2,1)}, u32[]{:S(2)}) copy-start(bf16[256,1152]{1,0:T(8,128)(2,1)} %constant.4.clone.sel_ref) | copy-start | bytes 1769476
  0.0 28.8 %copy-start = (bf16[189,20736]{1,0:T(8,128)(2,1)S(1)}, bf16[189,20736]{1,0:T(8,128)(2,1)}, u32[]{:S(2)}) copy-start(bf16[189,20736]{1,0:T(8,128)(2,1)} %table.1) | copy-start | bytes 23514628
  25.2 12.6 %slice-start = ((s8[5308416]{0:T(1024)(128)(4,1)}), s8[4194304]{0:T(1024)(128)(4,1)S(1)}, s32[]{:S(2)}) async-start(s8[5308416]{0:T(1024)(128)(4,1)} %bitcast.14), calls=%async_computation | async-start | bytes 8388608
  25.2 12.6 %slice-start.1 = ((s8[5308416]{0:T(1024)(128)(4,1)}), s8[1114112]{0:T(1024)(128)(4,1)S(1)}, s32[]{:S(2)}) async-start(s8[5308416]{0:T(1024)(128)(4,1)} %bitcast.14), calls=%async_computation.1 | async-start | bytes 2228224
  28.7 9.1 %copy-start.2 = (bf16[1152,256]{1,0:T(8,128)(2,1)S(1)}, bf16[1152,256]{1,0:T(8,128)(2,1)}, u32[]{:S(2)}) copy-start(bf16[1152,256]{1,0:T(8,128)(2,1)} %constant.5.clone.seg_ref) | copy-start | bytes 1769476
  28.7 9.1 %copy-start.3 = (f32[3,2048]{1,0:T(4,128)S(1)}, f32[3,2048]{1,0:T(4,128)}, u32[]{:S(2)}) copy-start(f32[3,2048]{1,0:T(4,128)} %param.14) | copy-start | bytes 73732
  28.7 9.1 %copy-start.4 = (s32[16,32]{1,0:T(8,128)S(1)}, s32[16,32]{1,0:T(8,128)}, u32[]{:S(2)}) copy-start(s32[16,32]{1,0:T(8,128)} %slot_ref.1) | copy-start | bytes 6148
  28.7 9.1 %copy-start.5 = (s32[16,32]{1,0:T(8,128)S(1)}, s32[16,32]{1,0:T(8,128)}, u32[]{:S(2)}) copy-start(s32[16,32]{1,0:T(8,128)} %class_ref.1) | copy-start | bytes 6148
  28.7 9.1 %copy-start.6 = (s32[1,128,4]{1,2,0:T(4,128)S(1)}, s32[1,128,4]{1,2,0:T(4,128)}, u32[]{:S(2)}) copy-start(s32[1,128,4]{1,2,0:T(4,128)} %param.20) | copy-start | bytes 6148
  28.8 9.1 %copy-start.7 = (s32[16]{0:T(128)S(1)}, s32[16]{0:T(128)}, u32[]{:S(2)}) copy-start(s32[16]{0:T(128)} %fcnt_ref.1) | copy-start | bytes 196

commit v4 on v3

--- a/solution.py
+++ b/solution.py
@@ -11,7 +11,6 @@
 
 KERNEL = 1.0 / (8.0 * math.pi)
 BLOB = 0.25
-PITCH = 9
 SIDE = 4
 F32 = jnp.float32
 BF16 = jnp.bfloat16
@@ -26,6 +25,7 @@
 def in_hbm(*arrays):
     return [pltpu.with_memory_space_constraint(a, pltpu.HBM) for a in arrays]
 
+UNROLL = 2
 EARLY = 4
 
 
@@ -115,9 +115,6 @@
     ]
     fill = jnp.zeros((8 - len(ends), 128), F32)
     own[...] = jnp.concatenate([main] + ends + [fill], axis=0).astype(BF16)
-    lax.fori_loop(0, leaves // 2, spread, 0)
-    racc[...] = jnp.zeros_like(racc)
-
     pl.semaphore_wait(barrier, chips + 1)
     to_partner = pltpu.make_async_remote_copy(
         src_ref=own,
@@ -168,6 +165,8 @@
             device_id=(target,),
             device_id_type=MESH,
         ).start()
+    lax.fori_loop(0, leaves // 2, spread, 0)
+    racc[...] = jnp.zeros_like(racc)
     for copy in halos:
         copy.wait()
 
@@ -285,6 +284,10 @@
     )(*in_hbm(near, cnt), wpos, wden, cols, racc, early)
 
 
+def class_pitch(chunks):
+    return chunks + 1 + chunks % 2
+
+
 def back_kernel(count, bef_ref, aft_ref, mom_ref, sel_ref, table, got, wide, pattern, send_sem, recv_sem):
     classes = table.shape[0]
     chunks = table.shape[1] // 128
@@ -332,22 +335,27 @@
 
     lax.fori_loop(0, mom_ref.shape[0] // 8, spread, 0)
 
+    pitch = class_pitch(chunks)
+
     def widen(block, _):
         rows = pl.ds(pl.multiple_of(block * 8, 8), 8)
-        at = block * (chunks * PITCH)
+        at = block * (8 * pitch)
         for chunk in range(chunks):
-            wide[pl.ds(at + chunk * PITCH, 8)] = table[rows, 128 * chunk : 128 * chunk + 128].astype(F32)
+            to = chunk % 9 * (chunks // 9) + chunk // 9
+            wide[pl.ds(at + to, 8, stride=pitch), :] = table[rows, 128 * chunk : 128 * chunk + 128].astype(F32)
         return 0
 
     full = classes // 8
     rest = classes - 8 * full
     lax.fori_loop(0, full, widen, 0)
     if rest:
-        at = full * chunks * PITCH
+        at = full * 8 * pitch
         for chunk in range(chunks):
-            wide[at + chunk * PITCH : at + chunk * PITCH + rest] = table[
+            to = chunk % 9 * (chunks // 9) + chunk // 9
+            wide[pl.ds(at + to, rest, stride=pitch), :] = table[
                 8 * full :, 128 * chunk : 128 * chunk + 128
             ].astype(F32)
+    pattern[:, mom_ref.shape[0] * 32 :] = jnp.zeros((9, 8, 128), F32)
     for copy in copies:
         copy.wait()
 
@@ -355,15 +363,15 @@
 def back_call(count, bef, aft, mom, table, width):
     leaves = bef.shape[0]
     chunks = table.shape[1] // 128
-    blocks = -(-table.shape[0] // 8)
+    rows = table.shape[0] * class_pitch(chunks) + 8
     sel, _ = constants(width)
     return pl.pallas_call(
         functools.partial(back_kernel, count),
         name="back",
         out_shape=(
             jax.ShapeDtypeStruct((2,) + bef.shape, F32),
-            jax.ShapeDtypeStruct(((blocks * chunks + 54) * PITCH, 128), F32),
-            jax.ShapeDtypeStruct((9, count * leaves, 128), F32),
+            jax.ShapeDtypeStruct((rows + -rows % 8, 128), F32),
+            jax.ShapeDtypeStruct((9, count * leaves + 8, 128), F32),
         ),
         in_specs=[VMEM] * 5,
         out_specs=(VMEM,) * 3,
@@ -378,33 +386,42 @@
 
 
 def far_kernel(
-    slot_ref, class_ref, fcnt_ref, req_ref, wide, pattern, seg_ref, basis, den_ref, tgt_ref, got, out_ref, sums
+    slot_ref, class_ref, fcnt_ref, req_ref, wide, pattern, seg_ref, basis, den_ref, tgt_ref, got, out_ref, sums, weight, down
 ):
     leaves, parts = basis.shape[0], basis.shape[1]
     width = basis.shape[2]
-    block_rows = width * width // 128 * PITCH
+    pitch = class_pitch(width * width // 128)
+    tall = width // 8
+    nothing = pattern.shape[1] - 8
+    slots = slot_ref.shape[1]
 
     def leaf_step(leaf, _):
+        live = fcnt_ref[leaf]
+
         def fetch(slot):
-            v = slot_ref[leaf, slot]
-            kind = class_ref[leaf, slot]
+            at = jnp.minimum(slot, slots - 1)
+            v = slot_ref[leaf, at]
             who = v >> 2
-            return who * leaves + req_ref[v & 3, who], (kind >> 3) * block_rows + (kind & 7)
-
-        def slot_step(slot, carry):
-            at, start, acc = carry
-            following = fetch(jnp.minimum(slot + 1, 31))
+            place = who * leaves + req_ref[v & 3, who]
+            return jnp.where(slot < live, place, nothing), class_ref[leaf, at] * pitch
+
+        def slot_step(step, carry):
+            now, acc = carry
+            following = tuple(fetch(UNROLL * (step + 1) + i) for i in range(UNROLL))
             new = []
             for v in range(9):
-                p = jnp.broadcast_to(pattern[v, pl.ds(at, 1), :], (8, 128))
+                p = [jnp.broadcast_to(pattern[v, pl.ds(a[0], 1), :], (8, 128)) for a in now]
                 for g in range(3):
-                    t = wide[pl.ds(start + (72 * g + v) * PITCH, 8, stride=9 * PITCH), :]
-                    new.append(acc[3 * v + g] + p * t)
-            return following[0], following[1], tuple(new)
+                    t = [wide[pl.ds(a[1] + tall * v + 8 * g, 8), :] for a in now]
+                    terms = [x * y for x, y in zip(p, t)]
+                    while len(terms) > 1:
+                        terms = [x + y for x, y in zip(terms[::2], terms[1::2])]
+                    new.append(acc[3 * v + g] + terms[0])
+            return following, tuple(new)
 
         zero = jnp.zeros((8, 128), F32)
-        at, start = fetch(0)
-        _, _, acc = lax.fori_loop(0, fcnt_ref[leaf], slot_step, (at, start, (zero,) * 27))
+        first = tuple(fetch(i) for i in range(UNROLL))
+        _, acc = lax.fori_loop(0, (live + UNROLL - 1) // UNROLL, slot_step, (first, (zero,) * 27))
         for v in range(9):
             for g in range(3):
                 rows = pl.ds(pl.multiple_of(leaf * 24 + 8 * g, 8), 8)
@@ -417,9 +434,9 @@
         total = sums[v]
         high = total.astype(BF16)
         low = (total - high.astype(F32)).astype(BF16)
-        part = seg_ref[128 * v : 128 * v + 128]
-        result = result + jnp.dot(high, part, preferred_element_type=F32)
-        result = result + jnp.dot(low, part, preferred_element_type=F32)
+        both = jnp.concatenate([high, low], axis=1)
+        part = seg_ref[256 * v : 256 * v + 256]
+        result = result + jnp.dot(both, part, preferred_element_type=F32)
     group = lax.broadcasted_iota(jnp.int32, (24, seg_ref.shape[1]), 0)
     lane = lax.broadcasted_iota(jnp.int32, (24, seg_ref.shape[1]), 1)
     keep = group == (lane >> 3)
@@ -427,13 +444,26 @@
     for leaf in range(leaves):
         mine = jnp.where(keep, result[24 * leaf : 24 * leaf + 24], 0.0)
         rows.append(jnp.sum(mine, axis=0, keepdims=True))
-    expansion = jnp.concatenate(rows, axis=0)[:, :width].astype(BF16)
-    row = lax.broadcasted_iota(jnp.int32, expansion.shape, 0)
-    field = [jnp.zeros((leaves, 128), F32) for _ in range(parts)]
+    expansion = jnp.concatenate(rows, axis=0)[:, :width].astype(BF16).astype(F32)
+    square = (width, width)
+    diagonal = lax.broadcasted_iota(jnp.int32, square, 0) == lax.broadcasted_iota(jnp.int32, square, 1)
+    ones = jnp.ones((width, 128), BF16)
     for leaf in range(leaves):
-        only = jnp.where(row == leaf, expansion, jnp.zeros_like(expansion))
+        only = jnp.where(diagonal, jnp.broadcast_to(expansion[leaf : leaf + 1], square), 0.0)
+        weight[leaf] = jnp.dot(only.astype(BF16), ones, preferred_element_type=F32)
+
+    def down_step(leaf, _):
         for q in range(parts):
-            field[q] = field[q] + jnp.dot(only, basis[leaf, q], preferred_element_type=F32)
+            part = [jnp.zeros((8, 128), F32) for _ in range(2)]
+            for r in range(width // 16):
+                d = basis[leaf, q, 16 * r : 16 * r + 16].astype(F32)
+                for i in range(2):
+                    part[i] = part[i] + d[8 * i : 8 * i + 8] * weight[leaf, 16 * r + 8 * i : 16 * r + 8 * i + 8]
+            down[q, pl.ds(leaf, 1)] = jnp.sum(part[0] + part[1], axis=0, keepdims=True)
+        return 0
+
+    lax.fori_loop(0, leaves, down_step, 0)
+    field = [down[q] for q in range(parts)]
     for k in range(3):
         far = den_ref[:, 0, :] * field[k]
         for c in range(1, 3):
@@ -448,6 +478,7 @@
     sel[:128] = place[None, :] == np.arange(128)[:, None]
     sel[128:] = (place[None, :] >= 128) & ((place[None, :] - 128) == np.arange(128)[:, None] % (width - 128))
     seg = (flat[:, None] // width == np.arange(256)[None, :] % 8).astype(np.float32)
+    seg = np.repeat(seg.reshape(9, 1, 128, 256), 2, axis=1).reshape(-1, 256)
     return [jnp.asarray(m, BF16) for m in (sel, seg)]
 
 
@@ -460,7 +491,11 @@
         out_shape=jax.ShapeDtypeStruct(den.shape, F32),
         in_specs=[SMEM] * 4 + [VMEM] * 7,
         out_specs=VMEM,
-        scratch_shapes=[pltpu.VMEM((9, leaves * 24, 128), F32)],
+        scratch_shapes=[
+            pltpu.VMEM((9, leaves * 24, 128), F32),
+            pltpu.VMEM((leaves, basis.shape[2], 128), F32),
+            pltpu.VMEM((basis.shape[1], leaves, 128), F32),
+        ],
         compiler_params=pltpu.CompilerParams(vmem_limit_bytes=LIMIT),
         cost_estimate=pl.CostEstimate(flops=10**8, bytes_accessed=10**7, transcendentals=0),
     )(slots, kinds, fcnt, requests, wide, pattern, seg, basis, den, tgt, got)

time: 48.4 us -> 45 us (0.930); the launches traced: 47.6 us -> 45 us
  Pallas kernels: 47.4 us -> 44.8 us
    pallas_call x1, Pallas kernels: 25.2 us -> 22 us  [exchange_call(): pl.pallas_call(functools.partial(exchange_kernel, count), name='exchange'...]
    pallas_call x1, Pallas kernels: 9.02 us -> 10.2 us  [back_call(): pl.pallas_call(functools.partial(back_kernel, count), name='back', out_sh...]
    pallas_call x1, Pallas kernels: 9.69 us -> 9.13 us  [far_call(): pl.pallas_call(far_kernel, name='far', out_shape=jax.ShapeDtypeStruct(den...]
where the time goes in v4:
time: 45 us
  Pallas kernels  44.8 us (100%)
    pallas_call x1, Pallas kernels, exchange_call(): pl.pallas_call(functools.partial(exchange_kernel, count), name='exchange'...  22 us
    pallas_call x1, Pallas kernels, back_call(): pl.pallas_call(functools.partial(back_kernel, count), name='back', out_sh...  10.2 us
    pallas_call x1, Pallas kernels, far_call(): pl.pallas_call(far_kernel, name='far', out_shape=jax.ShapeDtypeStruct(den...  9.13 us
    pallas_call x1, Pallas kernels, near_call(): pl.pallas_call(near_kernel, name='near', out_shape=(grad, grad, grad), in...  3.46 us

profile of v4, /device:TPU:0, one launch (start us, length us, event | category | flops | bytes accessed | tf_op | source)
XLA Modules:
  0.0 45.0 jit_solution(1095218893053686475)
XLA Ops:
  0.0 0.0 copy-start.2
  0.0 0.0 copy-start
  0.0 22.0 %exchange.1 = (f32[48,3,128]{2,1,0:T(4,128)S(1)}, f32[48,3,128]{2,1,0:T(4,128)S(1)}, bf16[64,40,128]{2,1,0:T(8,128)(2,1)S(1)}, f32[16,6,128,128]{3,2,1,0:T(8,128...) custom-call(s32[8,16]{1,0:T(8,128)} %bitcast.21, s32[16]{0:T(128)} %cnt_ref.3, ...), custom_call_target="tpu_custom_call" | custom-call | tf_op jit(solution)/shard_map/exchange/pallas_call | solution.py:195
  22.0 0.0 slice-start
  22.0 0.0 slice-start.1
  22.0 3.5 %near.1 = (f32[16,3,128]{2,1,0:T(4,128)S(1)}, f32[16,3,128]{2,1,0:T(4,128)S(1)}, f32[16,3,128]{2,1,0:T(4,128)S(1)}) custom-call(s32[8,16]{1,0:T(8,128)} %bitcast.22, s32[16]{0:T(128)} %cnt_ref.3, f32[48,3,128]{2,1,0:T(4,128)S(1)} %get-tuple-element.17.wpos_ref, f32[48,3,128]{2,1,0:T(4,128)S(1)} %get-tuple-element.18.wden_ref, ...), custom_call_target="tpu_custom_call" | custom-call | flops 100000000 | bytes 10000000 | tf_op jit(solution)/shard_map/near/pallas_call | solution.py:272
  25.5 0.0 copy-start.1
  25.5 0.0 copy-start.3
  25.5 0.0 copy-start.4
  25.5 0.0 copy-start.5
  25.5 0.0 copy-start.6
  25.5 0.0 copy-start.7
  25.5 0.0 copy-done.2
  25.6 0.0 copy-done
  25.6 10.2 %back.1 = (f32[2,16,3,128]{3,2,1,0:T(4,128)S(1)}, f32[30816,128]{1,0:T(8,128)S(1)}, f32[9,2056,128]{2,1,0:T(8,128)S(1)}) custom-call(f32[16,3,128]{2,1,0:T(4,128)S(1)} %get-tuple-element.22.bef_ref, f32[16,3,128]{2,1,0:T(4,128)S(1)} %get-tuple-element.23.aft_ref, bf16[64,40,128]{2,1,0:T(8,128)(2,1)S(1)} %get-tuple-element.24.mom_ref, ...), custom_call_target="tpu_custom_call" | custom-call | tf_op jit(solution)/shard_map/back/pallas_call | solution.py:368
  35.8 0.0 slice-done
  35.8 0.0 slice-done.1
  35.8 0.0 copy-done.1
  35.8 0.0 copy-done.3
  35.8 0.0 copy-done.4
  35.8 0.0 copy-done.5
  35.8 0.0 copy-done.6
  35.8 0.0 copy-done.7
  35.9 9.1 %far.1 = f32[16,3,128]{2,1,0:T(4,128)} custom-call(s32[16,32]{1,0:T(8,128)S(1)} %copy-done.4, s32[16,32]{1,0:T(8,128)S(1)} %copy-done.5, s32[16]{0:T(128)S(1)} %copy-done.7, s32[4,128]{1,0:T(4,128)S(1)} %bitcast.19, f32[30816,128]{1,0:T(8,128)S(1)} %get-tuple-element.25.wide, f32[9,2056,128]{2,1,0:T(8,128)S(1)} %get-tuple-element.26.pattern, ...), custom_call_target="tpu_custom_call" | custom-call | flops 100000000 | bytes 10000000 | tf_op jit(solution)/shard_map/far/pallas_call | solution.py:488
  (1 shorter events, 0.0 us)
Async XLA Ops:
  0.0 25.5 %copy-start.2 = (bf16[256,1152]{1,0:T(8,128)(2,1)S(1)}, bf16[256,1152]{1,0:T(8,128)(2,1)}, u32[]{:S(2)}) copy-start(bf16[256,1152]{1,0:T(8,128)(2,1)} %constant.4.clone.sel_ref) | copy-start | bytes 1769476
  0.0 25.6 %copy-start = (bf16[189,20736]{1,0:T(8,128)(2,1)S(1)}, bf16[189,20736]{1,0:T(8,128)(2,1)}, u32[]{:S(2)}) copy-start(bf16[189,20736]{1,0:T(8,128)(2,1)} %table.1) | copy-start | bytes 23514628
  22.0 13.8 %slice-start = ((s8[5308416]{0:T(1024)(128)(4,1)}), s8[4194304]{0:T(1024)(128)(4,1)S(1)}, s32[]{:S(2)}) async-start(s8[5308416]{0:T(1024)(128)(4,1)} %bitcast.14), calls=%async_computation | async-start | bytes 8388608
  22.0 13.8 %slice-start.1 = ((s8[5308416]{0:T(1024)(128)(4,1)}), s8[1114112]{0:T(1024)(128)(4,1)S(1)}, s32[]{:S(2)}) async-start(s8[5308416]{0:T(1024)(128)(4,1)} %bitcast.14), calls=%async_computation.1 | async-start | bytes 2228224
  25.5 10.3 %copy-start.1 = (bf16[2304,256]{1,0:T(8,128)(2,1)S(1)}, bf16[2304,256]{1,0:T(8,128)(2,1)}, u32[]{:S(2)}) copy-start(bf16[2304,256]{1,0:T(8,128)(2,1)} %constant.5.clone.seg_ref) | copy-start | bytes 3538948
  25.5 10.3 %copy-start.3 = (f32[3,2048]{1,0:T(4,128)S(1)}, f32[3,2048]{1,0:T(4,128)}, u32[]{:S(2)}) copy-start(f32[3,2048]{1,0:T(4,128)} %param.14) | copy-start | bytes 73732
  25.5 10.3 %copy-start.4 = (s32[16,32]{1,0:T(8,128)S(1)}, s32[16,32]{1,0:T(8,128)}, u32[]{:S(2)}) copy-start(s32[16,32]{1,0:T(8,128)} %slot_ref.1) | copy-start | bytes 6148
  25.5 10.3 %copy-start.5 = (s32[16,32]{1,0:T(8,128)S(1)}, s32[16,32]{1,0:T(8,128)}, u32[]{:S(2)}) copy-start(s32[16,32]{1,0:T(8,128)} %class_ref.1) | copy-start | bytes 6148
  25.5 10.3 %copy-start.6 = (s32[1,128,4]{1,2,0:T(4,128)S(1)}, s32[1,128,4]{1,2,0:T(4,128)}, u32[]{:S(2)}) copy-start(s32[1,128,4]{1,2,0:T(4,128)} %param.20) | copy-start | bytes 6148
  25.5 10.3 %copy-start.7 = (s32[16]{0:T(128)S(1)}, s32[16]{0:T(128)}, u32[]{:S(2)}) copy-start(s32[16]{0:T(128)} %fcnt_ref.1) | copy-start | bytes 196

commit v5 on v4

--- a/solution.py
+++ b/solution.py
@@ -19,14 +19,43 @@
 VMEM = pl.BlockSpec(memory_space=pltpu.VMEM)
 HBM = pl.BlockSpec(memory_space=pltpu.HBM)
 MIB = 1 << 20
-LIMIT = 8 * MIB
+LIMIT = 6 * MIB
 
 
 def in_hbm(*arrays):
     return [pltpu.with_memory_space_constraint(a, pltpu.HBM) for a in arrays]
 
-UNROLL = 2
-EARLY = 4
+UNROLL = 3
+EARLY = 3
+
+
+def class_pitch(chunks):
+    return chunks + 1 + chunks % 2
+
+
+def widen_table(table, wide):
+    classes = table.shape[0]
+    chunks = table.shape[1] // 128
+    pitch = class_pitch(chunks)
+
+    def widen(block, _):
+        rows = pl.ds(pl.multiple_of(block * 8, 8), 8)
+        at = block * (8 * pitch)
+        for chunk in range(chunks):
+            to = chunk % 9 * (chunks // 9) + chunk // 9
+            wide[pl.ds(at + to, 8, stride=pitch), :] = table[rows, 128 * chunk : 128 * chunk + 128].astype(F32)
+        return 0
+
+    full = classes // 8
+    rest = classes - 8 * full
+    lax.fori_loop(0, full, widen, 0)
+    if rest:
+        at = full * 8 * pitch
+        for chunk in range(chunks):
+            to = chunk % 9 * (chunks // 9) + chunk // 9
+            wide[pl.ds(at + to, rest, stride=pitch), :] = table[
+                8 * full :, 128 * chunk : 128 * chunk + 128
+            ].astype(F32)
 
 
 def pair_block(leaf, source_x, source_f, cols, racc):
@@ -55,8 +84,8 @@
 
 
 def exchange_kernel(
-    count, near_ref, cnt_ref, pos_ref, den_ref, up_hbm, wpos_ref, wden_ref, mom_ref, cols, racc, early_ref, up, own, theirs,
-    up_sem, pair_send, pair_recv, halo_send, halo_recv, send_sem, recv_sem
+    count, near_ref, cnt_ref, pos_ref, den_ref, up_hbm, table_hbm, wpos_ref, wden_ref, mom_ref, cols, racc, early_ref, wide,
+    table, up, own, theirs, up_sem, table_sem, pair_send, pair_recv, halo_send, halo_recv, send_sem, recv_sem
 ):
     leaves, width = up.shape[0], up.shape[1]
     plane = SIDE * SIDE
@@ -97,6 +126,8 @@
         return 0
 
     get_up.wait()
+    get_table = pltpu.make_async_copy(table_hbm, table, table_sem)
+    get_table.start()
     total = jnp.zeros((leaves, width), F32)
     for leaf in range(leaves):
         only = jnp.where(row == leaf, rounded, 0.0).astype(BF16)
@@ -167,6 +198,8 @@
         ).start()
     lax.fori_loop(0, leaves // 2, spread, 0)
     racc[...] = jnp.zeros_like(racc)
+    get_table.wait()
+    widen_table(table, wide)
     for copy in halos:
         copy.wait()
 
@@ -189,8 +222,9 @@
     pltpu.make_async_copy(moved, moved, recv_sem).wait()
 
 
-def exchange_call(count, near, cnt, pos, den, up):
+def exchange_call(count, near, cnt, pos, den, up, table):
     leaves, rows, lanes = pos.shape
+    height = table.shape[0] * class_pitch(table.shape[1] // 128) + 8
     window = jax.ShapeDtypeStruct((3 * leaves, rows, lanes), F32)
     return pl.pallas_call(
         functools.partial(exchange_kernel, count),
@@ -202,13 +236,16 @@
             jax.ShapeDtypeStruct((leaves, 6, 128, 128), F32),
             jax.ShapeDtypeStruct((leaves, 3, 128, 128), F32),
             jax.ShapeDtypeStruct((leaves, EARLY, 3, 128), F32),
+            jax.ShapeDtypeStruct((height + -height % 8, 128), F32),
         ),
-        in_specs=[SMEM, SMEM, VMEM, VMEM, HBM],
-        out_specs=(VMEM,) * 6,
+        in_specs=[SMEM, SMEM, VMEM, VMEM, HBM, HBM],
+        out_specs=(VMEM,) * 7,
         scratch_shapes=[
+            pltpu.VMEM(table.shape, BF16),
             pltpu.VMEM(up.shape, BF16),
             pltpu.VMEM((24, 128), BF16),
             pltpu.VMEM((24, 128), BF16),
+            pltpu.SemaphoreType.DMA,
             pltpu.SemaphoreType.DMA,
             pltpu.SemaphoreType.DMA,
             pltpu.SemaphoreType.DMA,
@@ -218,13 +255,13 @@
             pltpu.SemaphoreType.DMA,
         ],
         compiler_params=pltpu.CompilerParams(
-            collective_id=0, has_side_effects=True, vmem_limit_bytes=LIMIT
+            collective_id=0, has_side_effects=True, vmem_limit_bytes=12 * MIB
         ),
-    )(*in_hbm(near, cnt, pos, den, up))
-
-
-def near_kernel(near_ref, cnt_ref, wpos_ref, wden_ref, cols, before_acc, early_ref, tgt_ref, bef_ref, aft_ref, racc, sacc):
-    leaves = tgt_ref.shape[0]
+    )(*in_hbm(near, cnt, pos, den, up, table))
+
+
+def near_kernel(near_ref, cnt_ref, wpos_ref, wden_ref, cols, early_ref, bef_ref, aft_ref, racc, own_ref, sacc):
+    leaves = bef_ref.shape[0]
     shift = (lax.axis_index("patch") - 1) * leaves
     sacc[...] = jnp.zeros_like(sacc)
 
@@ -246,51 +283,44 @@
 
     lax.fori_loop(0, leaves, leaf_step, 0)
 
-    def gather(pair, _):
-        for sub in range(2):
-            leaf = pair * 2 + sub
-            for k in range(3):
-                turned = jnp.transpose(racc[leaf, k] + before_acc[leaf, k], (1, 0))
-                folded = turned[0:8]
-                for tile in range(1, 16):
-                    folded = folded + turned[8 * tile : 8 * tile + 8]
-                folded = folded - sacc[leaves + leaf, k]
-                row = pl.ds(k, 1)
-                tgt_ref[leaf, row] = jnp.sum(folded, axis=0, keepdims=True) * KERNEL
-                bef_ref[leaf, row] = jnp.sum(sacc[leaf, k], axis=0, keepdims=True) * -KERNEL
-                aft_ref[leaf, row] = (
-                    jnp.sum(sacc[2 * leaves + leaf, k], axis=0, keepdims=True) * -KERNEL
-                )
-        return 0
-
-    lax.fori_loop(0, leaves // 2, gather, 0)
-
-
-def near_call(near, cnt, wpos, wden, cols, racc, early):
+    for k in range(3):
+        own_ref[:, k] = sacc[leaves : 2 * leaves, k]
+
+    def gather(leaf, _):
+        for k in range(3):
+            row = pl.ds(k, 1)
+            bef_ref[leaf, row] = jnp.sum(sacc[leaf, k], axis=0, keepdims=True) * -KERNEL
+            aft_ref[leaf, row] = jnp.sum(sacc[2 * leaves + leaf, k], axis=0, keepdims=True) * -KERNEL
+        return 0
+
+    lax.fori_loop(0, leaves, gather, 0, unroll=4)
+
+
+def near_call(near, cnt, wpos, wden, cols, early):
     leaves = cnt.shape[0]
     grad = jax.ShapeDtypeStruct((leaves, 3, 128), F32)
     return pl.pallas_call(
         near_kernel,
         name="near",
-        out_shape=(grad, grad, grad),
-        in_specs=[SMEM] * 2 + [VMEM] * 5,
-        out_specs=(VMEM,) * 3,
+        out_shape=(
+            grad,
+            grad,
+            jax.ShapeDtypeStruct((leaves, 3, 128, 128), F32),
+            jax.ShapeDtypeStruct((leaves, 3, 8, 128), F32),
+        ),
+        in_specs=[SMEM] * 2 + [VMEM] * 4,
+        out_specs=(VMEM,) * 4,
         scratch_shapes=[
-            pltpu.VMEM((leaves, 3, 128, 128), F32),
             pltpu.VMEM((3 * leaves, 3, 8, 128), F32),
         ],
         compiler_params=pltpu.CompilerParams(vmem_limit_bytes=LIMIT),
         cost_estimate=pl.CostEstimate(flops=10**8, bytes_accessed=10**7, transcendentals=10**6),
-    )(*in_hbm(near, cnt), wpos, wden, cols, racc, early)
-
-
-def class_pitch(chunks):
-    return chunks + 1 + chunks % 2
-
-
-def back_kernel(count, bef_ref, aft_ref, mom_ref, sel_ref, table, got, wide, pattern, send_sem, recv_sem):
-    classes = table.shape[0]
-    chunks = table.shape[1] // 128
+    )(*in_hbm(near, cnt), wpos, wden, cols, early)
+
+
+def back_kernel(
+    count, bef_ref, aft_ref, mom_ref, sel_ref, first_acc, racc, own_ref, got, pattern, tgt_ref, send_sem, recv_sem
+):
     me = lax.axis_index("patch")
     before = (me + count - 1) % count
     after = (me + 1) % count
@@ -335,45 +365,37 @@
 
     lax.fori_loop(0, mom_ref.shape[0] // 8, spread, 0)
 
-    pitch = class_pitch(chunks)
-
-    def widen(block, _):
-        rows = pl.ds(pl.multiple_of(block * 8, 8), 8)
-        at = block * (8 * pitch)
-        for chunk in range(chunks):
-            to = chunk % 9 * (chunks // 9) + chunk // 9
-            wide[pl.ds(at + to, 8, stride=pitch), :] = table[rows, 128 * chunk : 128 * chunk + 128].astype(F32)
-        return 0
-
-    full = classes // 8
-    rest = classes - 8 * full
-    lax.fori_loop(0, full, widen, 0)
-    if rest:
-        at = full * 8 * pitch
-        for chunk in range(chunks):
-            to = chunk % 9 * (chunks // 9) + chunk // 9
-            wide[pl.ds(at + to, rest, stride=pitch), :] = table[
-                8 * full :, 128 * chunk : 128 * chunk + 128
-            ].astype(F32)
     pattern[:, mom_ref.shape[0] * 32 :] = jnp.zeros((9, 8, 128), F32)
+
+    def gather(pair, _):
+        for sub in range(2):
+            leaf = pair * 2 + sub
+            for k in range(3):
+                turned = jnp.transpose(racc[leaf, k] + first_acc[leaf, k], (1, 0))
+                folded = turned[0:8]
+                for tile in range(1, 16):
+                    folded = folded + turned[8 * tile : 8 * tile + 8]
+                folded = folded - own_ref[leaf, k]
+                tgt_ref[leaf, pl.ds(k, 1)] = jnp.sum(folded, axis=0, keepdims=True) * KERNEL
+        return 0
+
+    lax.fori_loop(0, racc.shape[0] // 2, gather, 0)
     for copy in copies:
         copy.wait()
 
 
-def back_call(count, bef, aft, mom, table, width):
+def back_call(count, bef, aft, mom, first, racc, own, width):
     leaves = bef.shape[0]
-    chunks = table.shape[1] // 128
-    rows = table.shape[0] * class_pitch(chunks) + 8
     sel, _ = constants(width)
     return pl.pallas_call(
         functools.partial(back_kernel, count),
         name="back",
         out_shape=(
             jax.ShapeDtypeStruct((2,) + bef.shape, F32),
-            jax.ShapeDtypeStruct((rows + -rows % 8, 128), F32),
             jax.ShapeDtypeStruct((9, count * leaves + 8, 128), F32),
+            jax.ShapeDtypeStruct(bef.shape, F32),
         ),
-        in_specs=[VMEM] * 5,
+        in_specs=[VMEM] * 7,
         out_specs=(VMEM,) * 3,
         scratch_shapes=[
             pltpu.SemaphoreType.DMA((2,)),
@@ -382,11 +404,11 @@
         compiler_params=pltpu.CompilerParams(
             collective_id=1, has_side_effects=True, vmem_limit_bytes=LIMIT
         ),
-    )(bef, aft, mom, sel, table)
+    )(bef, aft, mom, sel, first, racc, own)
 
 
 def far_kernel(
-    slot_ref, class_ref, fcnt_ref, req_ref, wide, pattern, seg_ref, basis, den_ref, tgt_ref, got, out_ref, sums, weight, down
+    slot_ref, class_ref, fcnt_ref, req_ref, wide, pattern, seg_ref, rep_ref, basis, den_ref, tgt_ref, got, out_ref, sums, weight, down
 ):
     leaves, parts = basis.shape[0], basis.shape[1]
     width = basis.shape[2]
@@ -413,10 +435,10 @@
                 p = [jnp.broadcast_to(pattern[v, pl.ds(a[0], 1), :], (8, 128)) for a in now]
                 for g in range(3):
                     t = [wide[pl.ds(a[1] + tall * v + 8 * g, 8), :] for a in now]
-                    terms = [x * y for x, y in zip(p, t)]
-                    while len(terms) > 1:
-                        terms = [x + y for x, y in zip(terms[::2], terms[1::2])]
-                    new.append(acc[3 * v + g] + terms[0])
+                    total = acc[3 * v + g]
+                    for x, y in zip(p, t):
+                        total = total + x * y
+                    new.append(total)
             return following, tuple(new)
 
         zero = jnp.zeros((8, 128), F32)
@@ -437,20 +459,10 @@
         both = jnp.concatenate([high, low], axis=1)
         part = seg_ref[256 * v : 256 * v + 256]
         result = result + jnp.dot(both, part, preferred_element_type=F32)
-    group = lax.broadcasted_iota(jnp.int32, (24, seg_ref.shape[1]), 0)
-    lane = lax.broadcasted_iota(jnp.int32, (24, seg_ref.shape[1]), 1)
-    keep = group == (lane >> 3)
-    rows = []
-    for leaf in range(leaves):
-        mine = jnp.where(keep, result[24 * leaf : 24 * leaf + 24], 0.0)
-        rows.append(jnp.sum(mine, axis=0, keepdims=True))
-    expansion = jnp.concatenate(rows, axis=0)[:, :width].astype(BF16).astype(F32)
-    square = (width, width)
-    diagonal = lax.broadcasted_iota(jnp.int32, square, 0) == lax.broadcasted_iota(jnp.int32, square, 1)
-    ones = jnp.ones((width, 128), BF16)
-    for leaf in range(leaves):
-        only = jnp.where(diagonal, jnp.broadcast_to(expansion[leaf : leaf + 1], square), 0.0)
-        weight[leaf] = jnp.dot(only.astype(BF16), ones, preferred_element_type=F32)
+    expansion = result.astype(BF16)
+    for w in range(8):
+        spread = jnp.dot(expansion, rep_ref[:, 128 * w : 128 * w + 128], preferred_element_type=F32)
+        weight[pl.ds(w, leaves * 24, stride=8), :] = spread
 
     def down_step(leaf, _):
         for q in range(parts):
@@ -458,7 +470,7 @@
             for r in range(width // 16):
                 d = basis[leaf, q, 16 * r : 16 * r + 16].astype(F32)
                 for i in range(2):
-                    part[i] = part[i] + d[8 * i : 8 * i + 8] * weight[leaf, 16 * r + 8 * i : 16 * r + 8 * i + 8]
+                    part[i] = part[i] + d[8 * i : 8 * i + 8] * weight[pl.ds(pl.multiple_of(leaf * 192, 8) + 16 * r + 8 * i, 8), :]
             down[q, pl.ds(leaf, 1)] = jnp.sum(part[0] + part[1], axis=0, keepdims=True)
         return 0
 
@@ -477,28 +489,29 @@
     place = flat % width
     sel[:128] = place[None, :] == np.arange(128)[:, None]
     sel[128:] = (place[None, :] >= 128) & ((place[None, :] - 128) == np.arange(128)[:, None] % (width - 128))
-    seg = (flat[:, None] // width == np.arange(256)[None, :] % 8).astype(np.float32)
-    seg = np.repeat(seg.reshape(9, 1, 128, 256), 2, axis=1).reshape(-1, 256)
+    seg = (flat[:, None] // width == np.arange(128)[None, :]).astype(np.float32)
+    seg = np.repeat(seg.reshape(9, 1, 128, 128), 2, axis=1).reshape(-1, 128)
     return [jnp.asarray(m, BF16) for m in (sel, seg)]
 
 
 def far_call(slots, kinds, fcnt, requests, wide, pattern, basis, den, tgt, got):
     leaves = den.shape[0]
     _, seg = constants(basis.shape[2])
+    rep = (np.arange(1024)[None, :] // 128 == np.arange(128)[:, None]).astype(np.float32)
     return pl.pallas_call(
         far_kernel,
         name="far",
         out_shape=jax.ShapeDtypeStruct(den.shape, F32),
-        in_specs=[SMEM] * 4 + [VMEM] * 7,
+        in_specs=[SMEM] * 4 + [VMEM] * 8,
         out_specs=VMEM,
         scratch_shapes=[
             pltpu.VMEM((9, leaves * 24, 128), F32),
-            pltpu.VMEM((leaves, basis.shape[2], 128), F32),
+            pltpu.VMEM((leaves * 192, 128), F32),
             pltpu.VMEM((basis.shape[1], leaves, 128), F32),
         ],
         compiler_params=pltpu.CompilerParams(vmem_limit_bytes=LIMIT),
         cost_estimate=pl.CostEstimate(flops=10**8, bytes_accessed=10**7, transcendentals=0),
-    )(slots, kinds, fcnt, requests, wide, pattern, seg, basis, den, tgt, got)
+    )(slots, kinds, fcnt, requests, wide, pattern, seg, jnp.asarray(rep, BF16), basis, den, tgt, got)
 
 
 def per_device(
@@ -523,9 +536,11 @@
 
     pos, den = by_leaf(positions), by_leaf(densities)
     near = near_src.T
-    wpos, wden, mom, cols, racc, early = exchange_call(count, near, near_count, pos, den, up_basis)
-    tgt, bef, aft = near_call(near, near_count, wpos, wden, cols, racc, early)
-    got, wide, pattern = back_call(count, bef, aft, mom, transfer_table, width)
+    wpos, wden, mom, cols, first, early, wide = exchange_call(
+        count, near, near_count, pos, den, up_basis, transfer_table
+    )
+    bef, aft, racc, own = near_call(near, near_count, wpos, wden, cols, early)
+    got, pattern, tgt = back_call(count, bef, aft, mom, first, racc, own, width)
     out = far_call(
         far_slot,
         far_class,

time: 45 us -> 42.4 us (0.942)
  Pallas kernels: 44.8 us -> 42 us
    pallas_call x1, Pallas kernels: 3.46 us -> 1.55 us  [near_call(): pl.pallas_call(near_kernel, name='near', out_shape=(grad, grad, jax.Shape...]
    pallas_call x1, Pallas kernels: 10.2 us -> 11.3 us  [back_call(): pl.pallas_call(functools.partial(back_kernel, count), name='back', out_sh...]
    pallas_call x1, Pallas kernels: 9.13 us -> 8.02 us  [far_call(): pl.pallas_call(far_kernel, name='far', out_shape=jax.ShapeDtypeStruct(den...]
    pallas_call x1, Pallas kernels: 22 us -> 21.1 us  [exchange_call(): pl.pallas_call(functools.partial(exchange_kernel, count), name='exchange'...]
where the time goes in v5:
time: 42.4 us; the launch traced here: 42.2 us
  Pallas kernels  42 us (99%)
    pallas_call x1, Pallas kernels, exchange_call(): pl.pallas_call(functools.partial(exchange_kernel, count), name='exchange'...  21.1 us
    pallas_call x1, Pallas kernels, back_call(): pl.pallas_call(functools.partial(back_kernel, count), name='back', out_sh...  11.3 us
    pallas_call x1, Pallas kernels, far_call(): pl.pallas_call(far_kernel, name='far', out_shape=jax.ShapeDtypeStruct(den...  8.02 us
    pallas_call x1, Pallas kernels, near_call(): pl.pallas_call(near_kernel, name='near', out_shape=(grad, grad, jax.Shape...  1.55 us

profile of v5, /device:TPU:0, one launch (start us, length us, event | category | flops | bytes accessed | tf_op | source)
XLA Modules:
  0.0 42.2 jit_solution(83247394227367965)
XLA Ops:
  0.0 0.0 copy-start
  0.0 21.1 %exchange.1 = (f32[48,3,128]{2,1,0:T(4,128)S(1)}, f32[48,3,128]{2,1,0:T(4,128)S(1)}, bf16[64,40,128]{2,1,0:T(8,128)(2,1)S(1)}, f32[16,6,128,128]{3,2,1,0:T(8,128...) custom-call(s32[8,16]{1,0:T(8,128)} %bitcast.21, s32[16]{0:T(128)} %cnt_ref.3, ...), custom_call_target="tpu_custom_call" | custom-call | tf_op jit(solution)/shard_map/exchange/pallas_call | solution.py:229
  21.1 0.0 slice-start
  21.1 0.0 copy-start.1
  21.1 0.0 copy-start.2
  21.1 0.0 copy-start.3
  21.2 0.0 copy-start.4
  21.2 0.0 copy-start.5
  21.2 0.0 copy-start.6
  21.2 0.0 copy-start.7
  21.2 1.6 %near.1 = (f32[16,3,128]{2,1,0:T(4,128)S(1)}, f32[16,3,128]{2,1,0:T(4,128)S(1)}, f32[16,3,128,128]{3,2,1,0:T(8,128)S(1)}, f32[16,3,8,128]{3,2,1,0:T(8,128)S(1)}) custom-call(s32[8,16]{1,0:T(8,128)} %bitcast.22, s32[16]{0:T(128)} %cnt_ref.3, f32[48,3,128]{2,1,0:T(4,128)S(1)} %get-tuple-element.20.wpos_ref, f32[48,3,128]{2,1,0:T(4,128)S(1)} %get-tuple-element.21.wden_ref, ...), custom_call_target="tpu_custom_call" | custom-call | flops 100000000 | bytes 10000000 | tf_op jit(solution)/shard_map/near/pallas_call | solution.py:302
  22.8 0.0 copy-done
  22.8 0.0 slice-start.1
  22.8 11.3 %back.1 = (f32[2,16,3,128]{3,2,1,0:T(4,128)S(1)}, f32[9,2056,128]{2,1,0:T(8,128)S(1)}, f32[16,3,128]{2,1,0:T(4,128)S(1)}) custom-call(f32[16,3,128]{2,1,0:T(4,128)S(1)} %get-tuple-element.24.bef_ref, f32[16,3,128]{2,1,0:T(4,128)S(1)} %get-tuple-element.25.aft_ref, bf16[64,40,128]{2,1,0:T(8,128)(2,1)S(1)} %get-tuple-element.26.mom_ref, ...), custom_call_target="tpu_custom_call" | custom-call | tf_op jit(solution)/shard_map/back/pallas_call | solution.py:390
  34.1 0.0 slice-done
  34.1 0.0 copy-done.1
  34.1 0.0 copy-done.2
  34.1 0.0 copy-done.3
  34.1 0.0 copy-done.4
  34.2 0.0 copy-done.5
  34.2 0.0 copy-done.6
  34.2 0.0 copy-done.7
  34.2 0.0 slice-done.1
  34.2 8.0 %far.1 = f32[16,3,128]{2,1,0:T(4,128)} custom-call(s32[16,32]{1,0:T(8,128)S(1)} %copy-done.4, s32[16,32]{1,0:T(8,128)S(1)} %copy-done.5, s32[16]{0:T(128)S(1)} %copy-done.7, s32[4,128]{1,0:T(4,128)S(1)} %bitcast.19, f32[30816,128]{1,0:T(8,128)S(1)} %get-tuple-element.19.wide, f32[9,2056,128]{2,1,0:T(8,128)S(1)} %get-tuple-element.30.pattern, ...), custom_call_target="tpu_custom_call" | custom-call | flops 100000000 | bytes 10000000 | tf_op jit(solution)/shard_map/far/pallas_call | solution.py:501
  (1 shorter events, 0.0 us)
Async XLA Ops:
  0.0 22.8 %copy-start = (bf16[256,1152]{1,0:T(8,128)(2,1)S(1)}, bf16[256,1152]{1,0:T(8,128)(2,1)}, u32[]{:S(2)}) copy-start(bf16[256,1152]{1,0:T(8,128)(2,1)} %constant.6.clone.sel_ref) | copy-start | bytes 1769476
  21.1 13.0 %slice-start = ((s8[5308416]{0:T(1024)(128)(4,1)}), s8[4194304]{0:T(1024)(128)(4,1)S(1)}, s32[]{:S(2)}) async-start(s8[5308416]{0:T(1024)(128)(4,1)} %bitcast.14), calls=%async_computation | async-start | bytes 8388608
  21.1 13.0 %copy-start.1 = (bf16[2304,128]{1,0:T(8,128)(2,1)S(1)}, bf16[2304,128]{1,0:T(8,128)(2,1)}, u32[]{:S(2)}) copy-start(bf16[2304,128]{1,0:T(8,128)(2,1)} %constant.7.clone.seg_ref) | copy-start | bytes 1769476
  21.1 13.0 %copy-start.2 = (bf16[128,1024]{1,0:T(8,128)(2,1)S(1)}, bf16[128,1024]{1,0:T(8,128)(2,1)}, u32[]{:S(2)}) copy-start(bf16[128,1024]{1,0:T(8,128)(2,1)} %constant.8.clone.rep_ref) | copy-start | bytes 786436
  21.1 13.0 %copy-start.3 = (f32[3,2048]{1,0:T(4,128)S(1)}, f32[3,2048]{1,0:T(4,128)}, u32[]{:S(2)}) copy-start(f32[3,2048]{1,0:T(4,128)} %param.15) | copy-start | bytes 73732
  21.2 13.0 %copy-start.4 = (s32[16,32]{1,0:T(8,128)S(1)}, s32[16,32]{1,0:T(8,128)}, u32[]{:S(2)}) copy-start(s32[16,32]{1,0:T(8,128)} %slot_ref.1) | copy-start | bytes 6148
  21.2 13.0 %copy-start.5 = (s32[16,32]{1,0:T(8,128)S(1)}, s32[16,32]{1,0:T(8,128)}, u32[]{:S(2)}) copy-start(s32[16,32]{1,0:T(8,128)} %class_ref.1) | copy-start | bytes 6148
  21.2 13.0 %copy-start.6 = (s32[1,128,4]{1,2,0:T(4,128)S(1)}, s32[1,128,4]{1,2,0:T(4,128)}, u32[]{:S(2)}) copy-start(s32[1,128,4]{1,2,0:T(4,128)} %param.21) | copy-start | bytes 6148
  21.2 13.0 %copy-start.7 = (s32[16]{0:T(128)S(1)}, s32[16]{0:T(128)}, u32[]{:S(2)}) copy-start(s32[16]{0:T(128)} %fcnt_ref.1) | copy-start | bytes 196
  22.8 11.4 %slice-start.1 = ((s8[5308416]{0:T(1024)(128)(4,1)}), s8[1114112]{0:T(1024)(128)(4,1)S(1)}, s32[]{:S(2)}) async-start(s8[5308416]{0:T(1024)(128)(4,1)} %bitcast.14), calls=%async_computation.1 | async-start | bytes 2228224
